TPU v7x, 128 devices: a whole 4x4x4 slice. The times are simulated.
128 devices in a mesh: sys: 1, zdom: 64 (over z, y, x), ydom: 2 (over core).
Axes of the slice: x: 4, y: 4, z: 4, core: 2. Of those that a mesh axis runs over, the one named last changes fastest.
Arguments:
- charge: float32 [2097152], P(('sys', 'ydom', 'zdom'))
- real_mask: int32 [2097152], P(('sys', 'ydom', 'zdom'))
- grid_idx: int32 [2097152, 3], P(('sys', 'ydom', 'zdom'))
- spline_w: float32 [2097152, 3, 4], P(('sys', 'ydom', 'zdom'))
- influence: float32 [256, 256, 256], P(('sys', 'ydom'), 'zdom')
Outputs:
- output 1: float32 [256, 256, 256], P(('sys', 'ydom'), 'zdom')
- output 2: float32 [1], P('sys')
All inputs are finite; a program needn't handle non-finite values.
Results may differ from a plain program's by a relative error of at most 0.001.
Values are sent between devices in bfloat16 or wider.
A program may use at most 1 GiB of HBM per device.

v0:
```python
import math
import jax
import jax.numpy as jnp
from jax import lax
from jax.sharding import PartitionSpec as P

PRECISE = lax.Precision.HIGHEST
GHOST_PLANES = 3


def tap_weights(base, taps_w, length):
    position = (base[..., None] + jnp.arange(4)) % length
    hit_mask = jnp.arange(length)[:, None] == position[..., None, :]
    return jnp.sum(jnp.where(hit_mask, taps_w[..., None, :], 0.0), axis=-1)


def spread_block(charge, real_mask, grid_idx, spline_w, grid_n, len_y, len_z):
    weight = charge * real_mask.astype(jnp.float32)
    line_x = tap_weights(grid_idx[..., 0], spline_w[..., 0, :], grid_n) * weight[..., None]
    line_y = tap_weights(grid_idx[..., 1], spline_w[..., 1, :], len_y + GHOST_PLANES)
    line_z = tap_weights(grid_idx[..., 2], spline_w[..., 2, :], len_z + GHOST_PLANES)
    plane_yz = line_y[..., :, None] * line_z[..., None, :]
    return jnp.einsum('...nx,...nyz->...xyz', line_x, plane_yz, precision=PRECISE, preferred_element_type=jnp.float32)


def dft_parts(grid_n, freq_rows):
    phase_idx = (freq_rows[:, None] * jnp.arange(grid_n)[None, :]) % grid_n
    angle_rad = phase_idx.astype(jnp.float32) * (2.0 * math.pi / grid_n)
    return jnp.cos(angle_rad), jnp.sin(angle_rad)


def real_dft(cos_part, sine_part):
    return jnp.stack([cos_part, -sine_part])


def complex_dft(cos_part, sine_part):
    return jnp.stack([jnp.stack([cos_part, sine_part]), jnp.stack([-sine_part, cos_part])])


def fold_ghosts(ext_block, axis_name, axis_size, axis_dim, length):
    ghost_slab = lax.slice_in_dim(ext_block, length, length + GHOST_PLANES, axis=axis_dim)
    recv_slab = lax.ppermute(ghost_slab, axis_name, [(source, (source + 1) % axis_size) for source in range(axis_size)])
    head_planes = lax.slice_in_dim(ext_block, 0, GHOST_PLANES, axis=axis_dim) + recv_slab
    rest_planes = lax.slice_in_dim(ext_block, GHOST_PLANES, length, axis=axis_dim)
    return jnp.concatenate([head_planes, rest_planes], axis=axis_dim)


def solution(mesh):
    y_devs = mesh.shape['ydom']
    z_devs = mesh.shape['zdom']
    slot_spec = P(('sys', 'ydom', 'zdom'))
    mode_spec = P(('sys', 'ydom'), 'zdom', None)

    def local_energy(charge, real_mask, grid_idx, spline_w, influence):
        grid_n = influence.shape[2]
        len_y = grid_n // y_devs
        len_z = grid_n // z_devs
        extended = spread_block(charge, real_mask, grid_idx, spline_w, grid_n, len_y, len_z)
        folded_y = fold_ghosts(extended, 'ydom', y_devs, 1, len_y)
        charge_grid = fold_ghosts(folded_y, 'zdom', z_devs, 2, len_z)
        cos_part, sine_part = dft_parts(grid_n, jnp.arange(grid_n))
        full_dft = complex_dft(cos_part, sine_part)
        stage_x = jnp.einsum('rkx,xyz->rkyz', real_dft(cos_part, sine_part), charge_grid, precision=PRECISE, preferred_element_type=jnp.float32)
        stage_x = lax.all_to_all(stage_x, 'ydom', 1, 2, tiled=True)
        stage_y = jnp.einsum('abky,bxyz->axkz', full_dft, stage_x, precision=PRECISE, preferred_element_type=jnp.float32)
        stage_y = lax.all_to_all(stage_y, 'zdom', 2, 3, tiled=True)
        stage_z = jnp.einsum('abkz,bxyz->axyk', full_dft, stage_y, precision=PRECISE, preferred_element_type=jnp.float32)
        mode_energy = 0.5 * influence * (stage_z[0] * stage_z[0] + stage_z[1] * stage_z[1])
        energy = lax.psum(jnp.sum(mode_energy), ('ydom', 'zdom')) / (grid_n * grid_n * grid_n)
        return mode_energy, jnp.reshape(energy, (1,))

    return jax.shard_map(local_energy, mesh=mesh, in_specs=(slot_spec, slot_spec, P(('sys', 'ydom', 'zdom'), None), P(('sys', 'ydom', 'zdom'), None, None), mode_spec), out_specs=(mode_spec, P('sys')), check_vma=False)
```

profile of v0, /device:TPU:1, one launch (start us, length us, event | category | flops | bytes accessed | tf_op | source)
XLA Modules:
  0.0 264.6 jit_solution(7145817684976135781)
XLA Ops:
  0.6 1.2 slice_bitcast_fusion.2
  1.8 1.4 fusion.51
  3.2 0.3 add_select_fusion.1
  3.5 0.3 add_select_fusion
  3.8 0.2 add_select_fusion.2
  4.0 26.3 %select_reduce_fusion.1 = f32[16384,131]{0,1:T(8,128)} fusion(f32[16384,4]{0,1:T(4,128)S(1)} %get-tuple-element.14, s32[16384,4]{0,1:T(4,128)S(1)} %add_select_fusion.1), kind=kLoop, calls=%fused_computation.4 | loop fusion | flops 23609344 | bytes 9109504 | tf_op jit(solution)/shard_map/reduce_sum | solution.py:14
  30.3 1.2 select_reduce_fusion.2
  31.5 0.0 copy-start
  31.6 0.0 copy-start.1
  31.6 22.7 %fusion.58 = f32[16384,131,7]{0,1,2:T(8,128)} fusion(f32[16384,7]{0,1:T(8,128)S(1)} %select_reduce_fusion.2, f32[16384,131]{0,1:T(8,128)} %select_reduce_fusion.1), kind=kLoop, calls=%fused_computation.3.clone.2 | loop fusion | flops 15024128 | bytes 69140480 | tf_op jit(solution)/shard_map/...nx,...nyz->...xyz/dot_general | solution.py:23
  54.3 28.8 %select_reduce_fusion = f32[16384,256]{1,0:T(8,128)} fusion(f32[16384,4]{0,1:T(4,128)S(1)} %get-tuple-element.12, s32[16384,4]{0,1:T(4,128)S(1)} %add_select_fusion.2), kind=kLoop, calls=%fused_computation | loop fusion | flops 46137344 | bytes 17301504 | tf_op jit(solution)/shard_map/reduce_sum | solution.py:14
  83.0 0.0 copy-done
  83.1 0.0 copy-done.1
  83.1 54.9 %fusion = f32[256,131,7]{0,1,2:T(8,128)S(1)} fusion(f32[16384,256]{1,0:T(8,128)} %select_reduce_fusion, f32[16384]{0:T(1024)S(1)} %convert_multiply_fusion, f32[16384,131,7]{0,1,2:T(8,128)} %fusion.58), kind=kOutput, calls=%fused_computation.2 | convolution fusion | flops 46158315520 | bytes 77878272 | tf_op jit(solution)/shard_map/...nx,...nyz->...xyz/dot_general | solution.py:23
  138.0 1.5 collective-permute-start
  139.5 0.1 slice.60
  139.5 0.8 collective-permute-done
  140.4 1.6 collective-permute-start.1
  141.9 1.0 fusion.42
  142.9 1.0 fusion.43
  144.0 0.1 fusion.12
  144.1 14.2 %collective-permute-done.1 = f32[256,128,3]{0,1,2:T(8,128)S(1)} collective-permute-done((f32[256,128,3]{0,1,2:T(8,128)S(1)}, f32[256,128,3]{0,1,2:T(8,128)S(1)}, u32[]{:S(2)}, u32[]{:S(2)}) %collective-permute-start.1) | collective-permute-done | bytes 393248 | tf_op jit(solution)/shard_map/ppermute | solution.py:42
  158.3 0.1 fusion.26
  158.3 1.0 fusion.10
  159.4 0.7 copy.39
  160.0 5.6 %all_to_all.36 = f32[2,256,128,4]{2,3,0,1:T(4,128)S(1)} all-to-all(f32[2,256,128,4]{2,3,0,1:T(4,128)S(1)} %copy.39), channel_id=1, replica_groups=mesh['sys'=1,'zdom'=64,'ydom'=2] {'ydom'}, dimensions={1} | all-to-all | bytes 2097152 | tf_op jit(solution)/shard_map/all_to_all | solution.py:64
  165.7 0.8 copy.62
  166.5 0.8 reshape.172
  167.3 1.9 convolution_bitcast_fusion.1
  169.2 0.8 copy.41
  170.0 23.3 %all_to_all.37 = f32[2,128,256,4]{1,0,3,2:T(2,128)S(1)} all-to-all(f32[2,128,256,4]{1,0,3,2:T(2,128)S(1)} %copy.41), channel_id=1, replica_groups=mesh['sys'=1,'zdom'=64,'ydom'=2] {'zdom'}, dimensions={2} | all-to-all | bytes 2097152 | tf_op jit(solution)/shard_map/all_to_all | solution.py:66
  193.3 0.2 copy.42
  193.5 0.7 copy.43
  194.2 3.5 %convolution_bitcast_fusion = f32[2,128,4,256]{3,1,0,2:T(8,128)S(1)} fusion(f32[2,128,4,256,1]{1,3,2,0,4:T(8,128)S(1)} %bitcast.63, f32[1,2,256,256]{3,2,1,0:T(8,128)S(1)} %get-tuple-element.16, f32[1,2,256,256]{3,2,1,0:T(8,128)S(1)} %get-tuple-element.15), kind=kOutput, calls=%fused_computation.13 | convolution fusion | flops 1610874880 | bytes 3145728 | tf_op jit(solution)/shard_map/abkz,bxyz->axyk/dot_general | solution.py:67
  197.6 1.8 fusion.49
  199.4 1.1 copy.45
  200.6 62.2 %psum.7 = f32[]{:T(128)} all-reduce(f32[]{:T(128)} %get-tuple-element.10), channel_id=1, replica_groups=mesh['sys'=1,'zdom'=64,'ydom'=2] {'ydom','zdom'}, use_global_device_ids=true, to_apply=%region_4.5 | all-reduce | flops 1 | bytes 8 | tf_op jit(solution)/shard_map/psum | solution.py:69
  (4 shorter events, 0.1 us)
Async XLA Ops:
  31.5 51.5 %copy-start = (f32[16384]{0:T(1024)S(1)}, f32[16384]{0:T(1024)}, u32[]{:S(2)}) copy-start(f32[16384]{0:T(1024)} %param.5) | copy-start | bytes 196612
  31.6 51.5 %copy-start.1 = (s32[16384]{0:T(1024)S(1)}, s32[16384]{0:T(1024)}, u32[]{:S(2)}) copy-start(s32[16384]{0:T(1024)} %param.6) | copy-start | bytes 196612
  138.0 2.3 collective-permute-start
  140.4 17.9 %collective-permute-start.1 = (f32[256,128,3]{0,1,2:T(8,128)S(1)}, f32[256,128,3]{0,1,2:T(8,128)S(1)}, u32[]{:S(2)}, u32[]{:S(2)}) collective-permute-start(f32[256,128,3]{0,1,2:T(8,128)S(1)} %fusion.24), channel_id=1, source_target_pairs={{0,2},{2,4},{4,6},{6,8},{8,10},{10,12},{12,14},{14,16},{16,18},{18... | collective-permute-start | bytes 1179656 | tf_op jit(solution)/shard_map/ppermute | solution.py:42
where the time goes:
time: 265 us
  blocking collectives  91.1 us (34%)
  other arithmetic  83.8 us (32%)
  matrix products  61.3 us (23%)
  waiting for transfers between devices  15 us (6%)
  local copies, waits for them, and re-layouts  7.8 us (3%)
  starting transfers between devices  3.05 us (1%)
    psum x1, blocking collectives, local_energy(): lax.psum(jnp.sum(mode_energy), ('ydom', 'zdom'))  62.2 us
    reduce_sum x3, other arithmetic, tap_weights(): return jnp.sum(jnp.where(hit_mask, taps_w[..., None, :], 0.0), axis=-1)  56.3 us
    dot_general x1, matrix products, spread_block(): jnp.einsum('...nx,...nyz->...xyz', line_x, plane_yz, precision=PRECISE, p...  54.9 us
    all_to_all x1, blocking collectives, local_energy(): stage_y = lax.all_to_all(stage_y, 'zdom', 2, 3, tiled=True)  23.3 us
    dot_general x1, other arithmetic, spread_block(): jnp.einsum('...nx,...nyz->...xyz', line_x, plane_yz, precision=PRECISE, p...  22.7 us
    ppermute x2, waiting for transfers between devices, fold_ghosts(): lax.ppermute(ghost_slab, axis_name, [(source, (source + 1) % axis_size) f...  15 us
    all_to_all x1, blocking collectives, local_energy(): stage_x = lax.all_to_all(stage_x, 'ydom', 1, 2, tiled=True)  5.62 us
  transfers between devices with their start and end apart: 2, of which 2 were waited for; matrix products, arithmetic and copies ran while one was open for 1% of the time, Pallas kernels for 0%

commit v1 on v0

--- a/solution.py
+++ b/solution.py
@@ -1,26 +1,98 @@
+import functools
 import math
 import jax
 import jax.numpy as jnp
 from jax import lax
+from jax.experimental import pallas as pl
+from jax.experimental.pallas import tpu as pltpu
 from jax.sharding import PartitionSpec as P
 
 PRECISE = lax.Precision.HIGHEST
 GHOST_PLANES = 3
-
-
-def tap_weights(base, taps_w, length):
-    position = (base[..., None] + jnp.arange(4)) % length
-    hit_mask = jnp.arange(length)[:, None] == position[..., None, :]
-    return jnp.sum(jnp.where(hit_mask, taps_w[..., None, :], 0.0), axis=-1)
+F32 = jnp.float32
+BF16 = jnp.bfloat16
+SUB = 256
+CHUNK = 1024
+
+
+def split_bf16(value):
+    high = value.astype(BF16)
+    return high, (value - high.astype(F32)).astype(BF16)
+
+
+def dot_t(lhs, rhs):
+    return lax.dot_general(lhs, rhs, (((1,), (1,)), ((), ())), preferred_element_type=F32)
+
+
+def spread_kernel(len_y, q_ref, m_ref, idx_ref, w_ref, out_ref, xh_ref, xl_ref, ph_ref, pl_ref):
+    grid_n = out_ref.shape[1]
+
+    @pl.when(pl.program_id(0) == 0)
+    def _():
+        out_ref[...] = jnp.zeros_like(out_ref)
+
+    total = None
+    for sub in range(CHUNK // SUB):
+        slot = sub % 2
+        cols = pl.ds(sub * SUB, SUB)
+        weight = q_ref[:, cols] * m_ref[:, cols].astype(F32)
+        tap = lax.broadcasted_iota(jnp.int32, (4, SUB), 0)
+        pos_x = ((idx_ref[0:1, cols] + tap) % grid_n).astype(F32).astype(BF16)
+        pos_y = idx_ref[1:2, cols] + tap
+        pos_z = idx_ref[2:3, cols] + tap
+        wxh, wxl = split_bf16(w_ref[0, :, cols] * weight)
+        wy = w_ref[1, :, cols]
+        wz = w_ref[2, :, cols]
+
+        row_x = lax.broadcasted_iota(jnp.int32, (grid_n, SUB), 0).astype(F32).astype(BF16)
+        line_h = jnp.zeros((grid_n, SUB), BF16)
+        line_l = jnp.zeros((grid_n, SUB), BF16)
+        for s in range(4):
+            hit = row_x == pos_x[s:s + 1]
+            line_h = jnp.where(hit, wxh[s:s + 1], line_h)
+            line_l = jnp.where(hit, wxl[s:s + 1], line_l)
+        xh_ref[slot] = line_h
+        xl_ref[slot] = line_l
+
+        row_8 = lax.broadcasted_iota(jnp.int32, (8, SUB), 0)
+        line_z = jnp.zeros((8, SUB), F32)
+        ghost_y = jnp.zeros((8, SUB), F32)
+        row_y = lax.broadcasted_iota(jnp.int32, (len_y, SUB), 0)
+        line_y = jnp.zeros((len_y, SUB), F32)
+        for t in range(4):
+            line_z = jnp.where(row_8 == pos_z[t:t + 1], wz[t:t + 1], line_z)
+            ghost_y = jnp.where(row_8 + len_y == pos_y[t:t + 1], wy[t:t + 1], ghost_y)
+            line_y = jnp.where(row_y == pos_y[t:t + 1], wy[t:t + 1], line_y)
+        for z in range(7):
+            high, low = split_bf16(line_y * line_z[z:z + 1])
+            ph_ref[slot, z * len_y:(z + 1) * len_y, :] = high
+            pl_ref[slot, z * len_y:(z + 1) * len_y, :] = low
+        ghosts = jnp.concatenate([line_z * ghost_y[g:g + 1] for g in range(3)] + [jnp.zeros((8, SUB), F32)], axis=0)
+        high, low = split_bf16(ghosts)
+        ph_ref[slot, 7 * len_y:, :] = high
+        pl_ref[slot, 7 * len_y:, :] = low
+
+        part = dot_t(ph_ref[slot], xh_ref[slot]) + dot_t(pl_ref[slot], xh_ref[slot]) + dot_t(ph_ref[slot], xl_ref[slot])
+        out_ref[...] += part
 
 
 def spread_block(charge, real_mask, grid_idx, spline_w, grid_n, len_y, len_z):
-    weight = charge * real_mask.astype(jnp.float32)
-    line_x = tap_weights(grid_idx[..., 0], spline_w[..., 0, :], grid_n) * weight[..., None]
-    line_y = tap_weights(grid_idx[..., 1], spline_w[..., 1, :], len_y + GHOST_PLANES)
-    line_z = tap_weights(grid_idx[..., 2], spline_w[..., 2, :], len_z + GHOST_PLANES)
-    plane_yz = line_y[..., :, None] * line_z[..., None, :]
-    return jnp.einsum('...nx,...nyz->...xyz', line_x, plane_yz, precision=PRECISE, preferred_element_type=jnp.float32)
+    slots = charge.shape[0]
+    rows = (len_z + 3) * len_y + 32
+    return pl.pallas_call(
+        functools.partial(spread_kernel, len_y),
+        grid=(slots // CHUNK,),
+        in_specs=[
+            pl.BlockSpec((1, CHUNK), lambda i: (0, i)),
+            pl.BlockSpec((1, CHUNK), lambda i: (0, i)),
+            pl.BlockSpec((3, CHUNK), lambda i: (0, i)),
+            pl.BlockSpec((3, 4, CHUNK), lambda i: (0, 0, i)),
+        ],
+        out_specs=pl.BlockSpec((rows, grid_n), lambda i: (0, 0)),
+        out_shape=jax.ShapeDtypeStruct((rows, grid_n), F32),
+        scratch_shapes=[pltpu.VMEM((2, grid_n, SUB), BF16), pltpu.VMEM((2, grid_n, SUB), BF16), pltpu.VMEM((2, rows, SUB), BF16), pltpu.VMEM((2, rows, SUB), BF16)],
+        name="spread",
+    )(charge.reshape(1, slots), real_mask.reshape(1, slots), grid_idx.T, jnp.transpose(spline_w, (1, 2, 0)))
 
 
 def dft_parts(grid_n, freq_rows):
@@ -45,6 +117,60 @@
     return jnp.concatenate([head_planes, rest_planes], axis=axis_dim)
 
 
+def sum_kernel(y_devs, z_devs, part_ref, out_ref, all_ref, send_sem, recv_sem):
+    my_y = lax.axis_index('ydom')
+    my_z = lax.axis_index('zdom')
+    devs = y_devs * z_devs
+    me = my_z * y_devs + my_y
+
+    def place(step):
+        other = lax.rem(me + step, devs)
+        return {'zdom': other // y_devs, 'ydom': lax.rem(other, y_devs)}
+
+    barrier = pltpu.get_barrier_semaphore()
+
+    @pl.loop(1, devs)
+    def _(step):
+        pl.semaphore_signal(barrier, inc=1, device_id=place(step), device_id_type=pl.DeviceIdType.MESH)
+
+    pl.semaphore_wait(barrier, devs - 1)
+
+    def copy_to(step):
+        return pltpu.make_async_remote_copy(src_ref=part_ref, dst_ref=all_ref.at[me], send_sem=send_sem.at[step], recv_sem=recv_sem.at[me], device_id=place(step), device_id_type=pl.DeviceIdType.MESH)
+
+    def copy_from(source):
+        return pltpu.make_async_remote_copy(src_ref=part_ref, dst_ref=all_ref.at[source], send_sem=send_sem.at[0], recv_sem=recv_sem.at[source], device_id=place(0), device_id_type=pl.DeviceIdType.MESH)
+
+    @pl.loop(1, devs)
+    def _(step):
+        copy_to(step).start()
+
+    all_ref[me] = part_ref[...]
+
+    @pl.loop(1, devs)
+    def _(step):
+        copy_from(lax.rem(me + step, devs)).wait_recv()
+
+    @pl.loop(1, devs)
+    def _(step):
+        copy_to(step).wait_send()
+
+    out_ref[...] = jnp.sum(all_ref[...], axis=0)
+
+
+def all_sum(tile, y_devs, z_devs):
+    devs = y_devs * z_devs
+    return pl.pallas_call(
+        functools.partial(sum_kernel, y_devs, z_devs),
+        out_shape=jax.ShapeDtypeStruct(tile.shape, F32),
+        in_specs=[pl.BlockSpec(memory_space=pltpu.VMEM)],
+        out_specs=pl.BlockSpec(memory_space=pltpu.VMEM),
+        scratch_shapes=[pltpu.VMEM((devs,) + tile.shape, F32), pltpu.SemaphoreType.DMA((devs,)), pltpu.SemaphoreType.DMA((devs,))],
+        compiler_params=pltpu.CompilerParams(collective_id=0, has_side_effects=True),
+        name="all_sum",
+    )(tile)
+
+
 def solution(mesh):
     y_devs = mesh.shape['ydom']
     z_devs = mesh.shape['zdom']
@@ -55,7 +181,11 @@
         grid_n = influence.shape[2]
         len_y = grid_n // y_devs
         len_z = grid_n // z_devs
-        extended = spread_block(charge, real_mask, grid_idx, spline_w, grid_n, len_y, len_z)
+        flat = spread_block(charge, real_mask, grid_idx, spline_w, grid_n, len_y, len_z)
+        planes = flat[:7 * len_y].reshape(7, len_y, grid_n)
+        ghosts = flat[7 * len_y:7 * len_y + 24].reshape(3, 8, grid_n)[:, :7]
+        extended = jnp.concatenate([planes, jnp.transpose(ghosts, (1, 0, 2))], axis=1)
+        extended = jnp.transpose(extended, (2, 1, 0))
         folded_y = fold_ghosts(extended, 'ydom', y_devs, 1, len_y)
         charge_grid = fold_ghosts(folded_y, 'zdom', z_devs, 2, len_z)
         cos_part, sine_part = dft_parts(grid_n, jnp.arange(grid_n))
@@ -66,7 +196,8 @@
         stage_y = lax.all_to_all(stage_y, 'zdom', 2, 3, tiled=True)
         stage_z = jnp.einsum('abkz,bxyz->axyk', full_dft, stage_y, precision=PRECISE, preferred_element_type=jnp.float32)
         mode_energy = 0.5 * influence * (stage_z[0] * stage_z[0] + stage_z[1] * stage_z[1])
-        energy = lax.psum(jnp.sum(mode_energy), ('ydom', 'zdom')) / (grid_n * grid_n * grid_n)
+        tile = jnp.sum(mode_energy.reshape(8, -1, 128), axis=1)
+        energy = jnp.sum(all_sum(tile, y_devs, z_devs)) / (grid_n * grid_n * grid_n)
         return mode_energy, jnp.reshape(energy, (1,))
 
     return jax.shard_map(local_energy, mesh=mesh, in_specs=(slot_spec, slot_spec, P(('sys', 'ydom', 'zdom'), None), P(('sys', 'ydom', 'zdom'), None, None), mode_spec), out_specs=(mode_spec, P('sys')), check_vma=False)

time: 265 us -> 129 us (0.49)
  other arithmetic: 83.8 us -> 5.83 us
  blocking collectives: 91.1 us -> 26.9 us
  Pallas kernels: 0 us -> 54.2 us
  matrix products: 61.3 us -> 7.37 us
  local copies, waits for them, and re-layouts: 7.8 us -> 14.3 us
    psum x1 -> x0, blocking collectives: 62.2 us -> none  [local_energy(): lax.psum(jnp.sum(mode_energy), ('ydom', 'zdom'))]
    reduce_sum x4 -> x2, other arithmetic: 58.1 us -> 1.92 us  [the longest x1 1.29 us: local_energy(): energy = jnp.sum(all_sum(tile, y_devs, z_devs)) / (grid_n * grid_n * grid_n)]
    dot_general x1 -> x0, matrix products: 54.9 us -> none  [spread_block(): jnp.einsum('...nx,...nyz->...xyz', line_x, plane_yz, precision=PRECISE, p...]
    pallas_call x0 -> x2, Pallas kernels: none -> 54.2 us  [the longest x1 33 us: spread_block(): pl.pallas_call(functools.partial(spread_kernel, len_y), grid=(slots // CH...]
    dot_general x1 -> x0, other arithmetic: 22.7 us -> none  [spread_block(): jnp.einsum('...nx,...nyz->...xyz', line_x, plane_yz, precision=PRECISE, p...]
  transfers between devices with their start and end apart: 2 -> 2, of which waited for: 2 -> 1; matrix products, arithmetic and copies ran while one was open for 1% -> 3% of each run, Pallas kernels for 0% -> 0%
where the time goes in v1:
time: 129 us
  Pallas kernels  54.2 us (42%)
  blocking collectives  26.9 us (21%)
  waiting for transfers between devices  14.6 us (11%)
  local copies, waits for them, and re-layouts  14.3 us (11%)
  matrix products  7.37 us (6%)
  other arithmetic  5.83 us (5%)
  starting transfers between devices  2.84 us (2%)
  between operations  2.58 us (2%)
    pallas_call x1, Pallas kernels, spread_block(): pl.pallas_call(functools.partial(spread_kernel, len_y), grid=(slots // CH...  33 us
    all_to_all x1, blocking collectives, local_energy(): stage_y = lax.all_to_all(stage_y, 'zdom', 2, 3, tiled=True)  21.8 us
    pallas_call x1, Pallas kernels, all_sum(): pl.pallas_call(functools.partial(sum_kernel, y_devs, z_devs), out_shape=j...  21.1 us
    ppermute x2, waiting for transfers between devices, fold_ghosts(): lax.ppermute(ghost_slab, axis_name, [(source, (source + 1) % axis_size) f...  14.6 us
    all_to_all x1, blocking collectives, local_energy(): stage_x = lax.all_to_all(stage_x, 'ydom', 1, 2, tiled=True)  5.06 us
    all_to_all x2, local copies, waits for them, and re-layouts, local_energy(): stage_x = lax.all_to_all(stage_x, 'ydom', 1, 2, tiled=True)  3.84 us
    dot_general x1, matrix products, local_energy(): jnp.einsum('abkz,bxyz->axyk', full_dft, stage_y, precision=PRECISE, prefe...  3.47 us
    ppermute x2, starting transfers between devices, fold_ghosts(): lax.ppermute(ghost_slab, axis_name, [(source, (source + 1) % axis_size) f...  2.84 us
  transfers between devices with their start and end apart: 2, of which 1 were waited for; matrix products, arithmetic and copies ran while one was open for 3% of the time, Pallas kernels for 0%

profile of v1, /device:TPU:1, one launch (start us, length us, event | category | flops | bytes accessed | tf_op | source)
XLA Modules:
  0.0 128.5 jit_solution(1696314754491160098)
XLA Ops:
  0.6 33.0 %spread.1 = f32[928,256]{1,0:T(8,128)} custom-call(f32[1,16384]{1,0:T(1,128)} %bitcast.66, s32[1,16384]{1,0:T(1,128)} %bitcast.67, s32[3,16384]{1,0:T(4,128)} %bitcast.64, f32[3,4,16384]{2,1,0:T(4,128)} %bitcast.63), custom_call_target="tpu_custom_call" | custom-call | tf_op jit(solution)/shard_map/spread/pallas_call | solution.py:82
  33.7 0.0 copy-start
  33.7 0.0 slice-start
  33.7 1.2 copy-done
  34.9 0.3 slice-done
  35.2 0.3 copy.24
  35.5 1.3 copy.43
  36.7 1.3 %maximum_bitcast_fusion = f32[256,131,7]{1,0,2:T(8,128)S(1)} fusion(f32[7,3,256]{1,2,0:T(8,128)} %bitcast.62, f32[7,128,256]{1,2,0:T(8,128)S(1)} %copy.24), kind=kLoop, calls=%fused_computation | loop fusion | flops 234752 | bytes 1878016 | tf_op jit(solution)/shard_map/transpose | solution.py:188
  38.0 1.1 fusion.35
  39.1 0.3 copy.25
  39.5 1.4 %collective-permute-start = (f32[256,3,7]{0,2,1:T(8,128)S(1)}, f32[256,3,7]{0,2,1:T(8,128)S(1)}, u32[]{:S(2)}, u32[]{:S(2)}) collective-permute-start(f32[256,3,7]{0,2,1:T(8,128)S(1)} %copy.25), channel_id=1, source_target_pairs={{0,1},{1,0},{2,3},{3,2},{4,5},{5,4},{6,7},{7,6},{8,9},{9,8},{10,11... | collective-permute-start | bytes 64520 | tf_op jit(solution)/shard_map/ppermute | solution.py:114
  40.9 0.3 slice.51
  41.2 1.5 %copy.26 = f32[256,3,7]{0,2,1:T(8,128)S(1)} copy(f32[256,3,7]{1,0,2:T(8,128)} %get-tuple-element.9) | data formatting | bytes 43008 | tf_op jit(solution)/shard_map/slice | solution.py:115
  42.7 0.0 collective-permute-done
  42.7 0.3 copy.27
  43.1 0.2 fusion.17
  43.2 1.4 %collective-permute-start.1 = (f32[256,128,3]{1,0,2:T(8,128)S(1)}, f32[256,128,3]{1,0,2:T(8,128)S(1)}, u32[]{:S(2)}, u32[]{:S(2)}) collective-permute-start(f32[256,128,3]{1,0,2:T(8,128)S(1)} %fusion.17), channel_id=1, source_target_pairs={{0,2},{2,4},{4,6},{6,8},{8,10},{10,12},{12,14},{14,16},{16,18},{18... | collective-permute-start | bytes 1179656 | tf_op jit(solution)/shard_map/ppermute | solution.py:114
  44.7 1.0 fusion.28
  45.6 1.0 fusion.29
  46.7 0.1 fusion.5
  46.8 14.6 %collective-permute-done.1 = f32[256,128,3]{1,0,2:T(8,128)S(1)} collective-permute-done((f32[256,128,3]{1,0,2:T(8,128)S(1)}, f32[256,128,3]{1,0,2:T(8,128)S(1)}, u32[]{:S(2)}, u32[]{:S(2)}) %collective-permute-start.1) | collective-permute-done | bytes 393248 | tf_op jit(solution)/shard_map/ppermute | solution.py:114
  61.3 0.2 fusion.19
  61.5 1.1 fusion.3
  62.6 0.7 copy.28
  63.3 5.1 %all_to_all.36 = f32[2,256,128,4]{2,3,0,1:T(4,128)S(1)} all-to-all(f32[2,256,128,4]{2,3,0,1:T(4,128)S(1)} %copy.28), channel_id=1, replica_groups=mesh['sys'=1,'zdom'=64,'ydom'=2] {'ydom'}, dimensions={1} | all-to-all | bytes 2097152 | tf_op jit(solution)/shard_map/all_to_all | solution.py:194
  68.3 1.8 %copy.50 = f32[2,2,128,128,4]{3,1,2,0,4:T(2,128)} copy(f32[2,2,128,128,4]{3,4,0,2,1:T(4,128)S(1)} %bitcast.58) | data formatting | bytes 2097152 | tf_op jit(solution)/shard_map/all_to_all | solution.py:194
  70.1 2.1 %reshape.111 = f32[2,128,256,4,1]{2,1,0,3,4:T(8,128)S(1)} reshape(f32[2,128,2,128,4]{3,2,1,0,4:T(2,128)} %bitcast.59) | data formatting | bytes 2097152 | tf_op jit(solution)/shard_map/all_to_all | solution.py:194
  72.2 2.8 %convolution_bitcast_fusion.1 = f32[2,128,256,4]{2,1,0,3:T(8,128)} fusion(f32[2,128,256,4,1]{2,1,0,3,4:T(8,128)S(1)} %reshape.111, f32[1,2,256,256]{3,2,1,0:T(8,128)S(1)} %get-tuple-element.11, f32[1,2,256,256]{3,2,1,0:T(8,128)S(1)} %get-tuple-element.10), kind=kOutput, calls=%fused_computation.2 | convolution fusion | flops 1610874880 | bytes 3145728 | tf_op jit(solution)/shard_map/abky,bxyz->axkz/dot_general | solution.py:195
  75.0 1.7 %copy.30 = f32[2,128,256,4]{1,0,3,2:T(2,128)S(1)} copy(f32[2,128,256,4]{2,1,0,3:T(8,128)} %convolution_bitcast_fusion.1) | data formatting | bytes 2097152 | tf_op jit(solution)/shard_map/abky,bxyz->axkz/transpose | solution.py:195
  76.8 21.8 %all_to_all.37 = f32[2,128,256,4]{1,0,3,2:T(2,128)S(1)} all-to-all(f32[2,128,256,4]{1,0,3,2:T(2,128)S(1)} %copy.30), channel_id=1, replica_groups=mesh['sys'=1,'zdom'=64,'ydom'=2] {'zdom'}, dimensions={2} | all-to-all | bytes 2097152 | tf_op jit(solution)/shard_map/all_to_all | solution.py:196
  98.6 0.2 copy.31
  98.8 0.7 copy.32
  99.4 0.0 copy-start.2
  99.5 3.5 %convolution_bitcast_fusion = f32[2,128,4,256]{3,1,0,2:T(8,128)S(1)} fusion(f32[2,128,4,256,1]{1,3,2,0,4:T(8,128)S(1)} %bitcast.57, f32[1,2,256,256]{3,2,1,0:T(8,128)S(1)} %get-tuple-element.11, f32[1,2,256,256]{3,2,1,0:T(8,128)S(1)} %get-tuple-element.10), kind=kOutput, calls=%fused_computation.1 | convolution fusion | flops 1610874880 | bytes 3145728 | tf_op jit(solution)/shard_map/abkz,bxyz->axyk/dot_general | solution.py:197
  102.9 0.0 copy-done.2
  102.9 0.2 fusion.8
  103.1 0.3 copy.35
  103.5 0.0 copy-start.1
  103.5 0.2 reshape.107
  103.7 0.6 reduce_sum.18.part_ref
  104.3 21.1 %all_sum.1 = f32[8,128]{1,0:T(8,128)} custom-call(f32[8,128]{1,0:T(8,128)} %reduce_sum.18.part_ref), custom_call_target="tpu_custom_call" | custom-call | tf_op jit(solution)/shard_map/all_sum/pallas_call | solution.py:163
  125.5 1.3 %reduce_sum.19 = f32[]{:T(128)} reduce(f32[8,128]{1,0:T(8,128)} %all_sum.1, f32[]{:T(128)} %constant.22.clone.1), dimensions={0,1}, to_apply=%region_1.2 | reduce | flops 1023 | bytes 4104 | tf_op jit(solution)/shard_map/reduce_sum | solution.py:200
  127.4 0.0 copy-done.1
  (2 shorter events, 0.0 us)
Async XLA Ops:
  33.7 1.2 copy-start
  33.7 1.5 %slice-start = ((f32[928,256]{1,0:T(8,128)}), f32[896,256]{1,0:T(8,128)S(1)}, s32[]{:S(2)}) async-start(f32[928,256]{1,0:T(8,128)} %spread.1), calls=%async_computation.2 | async-start | bytes 1835008 | tf_op jit(solution)/shard_map/slice | solution.py:185
  39.5 3.2 %collective-permute-start = (f32[256,3,7]{0,2,1:T(8,128)S(1)}, f32[256,3,7]{0,2,1:T(8,128)S(1)}, u32[]{:S(2)}, u32[]{:S(2)}) collective-permute-start(f32[256,3,7]{0,2,1:T(8,128)S(1)} %copy.25), channel_id=1, source_target_pairs={{0,1},{1,0},{2,3},{3,2},{4,5},{5,4},{6,7},{7,6},{8,9},{9,8},{10,11... | collective-permute-start | bytes 64520 | tf_op jit(solution)/shard_map/ppermute | solution.py:114
  43.2 18.1 %collective-permute-start.1 = (f32[256,128,3]{1,0,2:T(8,128)S(1)}, f32[256,128,3]{1,0,2:T(8,128)S(1)}, u32[]{:S(2)}, u32[]{:S(2)}) collective-permute-start(f32[256,128,3]{1,0,2:T(8,128)S(1)} %fusion.17), channel_id=1, source_target_pairs={{0,2},{2,4},{4,6},{6,8},{8,10},{10,12},{12,14},{14,16},{16,18},{18... | collective-permute-start | bytes 1179656 | tf_op jit(solution)/shard_map/ppermute | solution.py:114
  99.4 3.5 %copy-start.2 = (f32[128,4,256]{2,1,0:T(4,128)S(1)}, f32[128,4,256]{2,1,0:T(4,128)}, u32[]{:S(2)}) copy-start(f32[128,4,256]{2,1,0:T(4,128)} %param.9) | copy-start | bytes 1572868
  103.5 24.0 %copy-start.1 = (f32[128,4,256]{2,1,0:T(4,128)}, f32[128,4,256]{2,1,0:T(4,128)S(1)}, u32[]{:S(2)}) copy-start(f32[128,4,256]{2,1,0:T(4,128)S(1)} %copy.35) | copy-start | bytes 1572868

commit v2 on v0

v2 whole, which is shorter than its diff:
```python
import functools
import math
import jax
import jax.numpy as jnp
import numpy as np
from jax import lax
from jax.experimental import pallas as pl
from jax.experimental.pallas import tpu as pltpu
from jax.sharding import PartitionSpec as P

F32 = jnp.float32
BF16 = jnp.bfloat16
SUB = 256
CHUNK = 1024
GROUPS = ((0, 1), (2, 3), (4, 5), (6,))
STEP_AT = 5
CODE_MAX = 32767.0
MESH = pl.DeviceIdType.MESH


def split_bf16(value):
    high = value.astype(BF16)
    return high, (value - high.astype(F32)).astype(BF16)


def dot3(lhs, rhs):
    def dot(a, b):
        return jnp.dot(a, b, preferred_element_type=F32)
    return dot(lhs[0], rhs[0]) + dot(lhs[1], rhs[0]) + dot(lhs[0], rhs[1])


def np_split(value):
    value = np.asarray(value, np.float32)
    high = value.astype(BF16)
    return np.stack([high, (value - high.astype(np.float32)).astype(BF16)])


def dft_tables(grid_n, y_devs, z_devs):
    turn = 2.0 * np.pi / grid_n
    len_y, len_z = grid_n // y_devs, grid_n // z_devs
    x = np.arange(grid_n)
    freq = np.arange(grid_n)
    phase_x = (np.outer(x, freq) % grid_n) * turn
    table_x = np.stack([np_split(np.concatenate([np.cos(phase_x[:, i * len_y:(i + 1) * len_y]), -np.sin(phase_x[:, i * len_y:(i + 1) * len_y])], axis=1)) for i in range(y_devs)])
    phase_y = (np.outer(freq, x) % grid_n) * turn
    real = np.concatenate([np.cos(phase_y), np.sin(phase_y)], axis=1)
    imag = np.concatenate([-np.sin(phase_y), np.cos(phase_y)], axis=1)
    rows = np.stack([real.reshape(z_devs, len_z, 2 * grid_n), imag.reshape(z_devs, len_z, 2 * grid_n)], axis=1)
    table_y = np_split(rows.reshape(2 * grid_n, 2 * grid_n))
    table_z = []
    for first in (0, 2):
        pos = np.arange(z_devs)[:, None] * len_z + first + np.arange(2)[None, :]
        phase_z = ((freq[:, None, None] * pos[None]) % grid_n) * turn
        real = np.stack([np.cos(phase_z), np.sin(phase_z)], axis=3).reshape(grid_n, -1)
        imag = np.stack([-np.sin(phase_z), np.cos(phase_z)], axis=3).reshape(grid_n, -1)
        table_z.append(np_split(np.concatenate([real, imag], axis=0)))
    return table_x, table_y, np.stack(table_z)


def energy_kernel(y_devs, z_devs, q_ref, m_ref, idx_ref, w_ref, bc_hbm, tx_hbm, ty_hbm, tz_hbm, ek_hbm, sum_ref,
                  xh_ref, xl_ref, ph_ref, pl_ref, acc_ref, got_ref, grid_ref, mid_ref, code_ref, recv_ref, scale_ref, rscale_ref,
                  deq_ref, zed_ref, bc_ref, ek_ref, tx_ref, ty_ref, tz_ref, row_ref, rrow_ref,
                  load_sem, swap_sem, send_sem, recv_sem, ssend_sem, srecv_sem, row_sem):
    my_y = lax.axis_index('ydom')
    my_z = lax.axis_index('zdom')
    grid_n = xh_ref.shape[1]
    slots = q_ref.shape[1]
    len_y = grid_n // y_devs
    n_groups = len(GROUPS)
    barrier = pltpu.get_barrier_semaphore()
    partner = {'ydom': 1 - my_y}

    def chip(step):
        return (my_z + step) & (z_devs - 1)

    @pl.loop(1, z_devs)
    def _(step):
        pl.semaphore_signal(barrier, inc=1, device_id={'zdom': chip(step)}, device_id_type=MESH)

    pl.semaphore_signal(barrier, inc=1, device_id=partner, device_id_type=MESH)

    loads = [pltpu.make_async_copy(tx_hbm.at[my_y], tx_ref, load_sem.at[0]), pltpu.make_async_copy(ty_hbm, ty_ref, load_sem.at[1]),
             pltpu.make_async_copy(tz_hbm, tz_ref, load_sem.at[2]), pltpu.make_async_copy(bc_hbm, bc_ref, load_sem.at[3])]
    for load in loads:
        load.start()

    def swap(group):
        return pltpu.make_async_remote_copy(src_ref=acc_ref.at[group], dst_ref=got_ref.at[group], send_sem=swap_sem.at[0, group], recv_sem=swap_sem.at[1, group], device_id=partner, device_id_type=MESH)

    def send(group, step):
        other = chip(step)
        return (pltpu.make_async_remote_copy(src_ref=code_ref.at[group, other], dst_ref=recv_ref.at[group, my_z], send_sem=send_sem.at[group], recv_sem=recv_sem.at[group], device_id={'zdom': other}, device_id_type=MESH),
                pltpu.make_async_remote_copy(src_ref=scale_ref.at[group, pl.ds(0, 1)], dst_ref=rscale_ref.at[group, my_z, pl.ds(0, 1)], send_sem=ssend_sem.at[group], recv_sem=srecv_sem.at[group], device_id={'zdom': other}, device_id_type=MESH))

    def spread(group, base):
        planes = GROUPS[group]
        total = None
        for sub in range(CHUNK // SUB):
            slot = sub % 2
            cols = pl.ds(pl.multiple_of(base + sub * SUB, SUB), SUB)
            tap = lax.broadcasted_iota(jnp.int32, (4, SUB), 0)
            if group == 0:
                weight = q_ref[:, cols] * m_ref[:, cols].astype(F32)
                pos_x = ((idx_ref[0:1, cols] + tap) & (grid_n - 1)).astype(F32).astype(BF16)
                wxh, wxl = split_bf16(w_ref[0, :, cols] * weight)
                row_x = lax.broadcasted_iota(jnp.int32, (grid_n, SUB), 0).astype(F32).astype(BF16)
                line_h = jnp.zeros((grid_n, SUB), BF16)
                line_l = jnp.zeros((grid_n, SUB), BF16)
                for s in range(4):
                    hit = row_x == pos_x[s:s + 1]
                    line_h = jnp.where(hit, wxh[s:s + 1], line_h)
                    line_l = jnp.where(hit, wxl[s:s + 1], line_l)
                xh_ref[cols, :] = line_h.T
                xl_ref[cols, :] = line_l.T
            pos_y = idx_ref[1:2, cols] + tap
            pos_z = idx_ref[2:3, cols] + tap
            wy = w_ref[1, :, cols]
            wz = w_ref[2, :, cols]
            row_8 = lax.broadcasted_iota(jnp.int32, (8, SUB), 0)
            line_z = jnp.zeros((8, SUB), F32)
            ghost_y = jnp.zeros((8, SUB), F32)
            row_y = lax.broadcasted_iota(jnp.int32, (len_y, SUB), 0)
            line_y = jnp.zeros((len_y, SUB), F32)
            for t in range(4):
                line_z = jnp.where(row_8 == pos_z[t:t + 1], wz[t:t + 1], line_z)
                ghost_y = jnp.where(row_8 + len_y == pos_y[t:t + 1], wy[t:t + 1], ghost_y)
                line_y = jnp.where(row_y == pos_y[t:t + 1], wy[t:t + 1], line_y)
            for k, z in enumerate(planes):
                high, low = split_bf16(line_y * line_z[z:z + 1])
                ph_ref[slot, k * len_y:(k + 1) * len_y, :] = high
                pl_ref[slot, k * len_y:(k + 1) * len_y, :] = low
            ghosts = [ghost_y * line_z[z:z + 1] for z in planes]
            if len(planes) == 1:
                ghosts.append(jnp.zeros((8, SUB), F32))
            high, low = split_bf16(jnp.concatenate(ghosts, axis=0))
            top = len(planes) * len_y
            ph_ref[slot, top:top + 16, :] = high
            pl_ref[slot, top:top + 16, :] = low
            rows = pl.ds(0, top + 16)
            part = dot3((ph_ref[slot, rows, :], pl_ref[slot, rows, :]), (xh_ref[cols, :], xl_ref[cols, :]))
            total = part if total is None else total + part
        acc_ref[group, rows, :] += total

    def transform_send(group):
        planes = GROUPS[group]
        swap(group).wait()
        mine, theirs = my_y * len_y, (1 - my_y) * len_y
        for k in range(len(planes)):
            block = pl.ds(k * len_y, len_y)
            grid_ref[pl.ds(pl.multiple_of(k * grid_n + mine, len_y), len_y), :] = acc_ref[group, block, :]
            grid_ref[pl.ds(pl.multiple_of(k * grid_n + theirs, len_y), len_y), :] = got_ref[group, block, :]
        for k in range(len(planes)):
            ghost = pl.ds(len(planes) * len_y + 8 * k, 8)
            grid_ref[pl.ds(pl.multiple_of(k * grid_n + theirs, len_y), 8), :] += acc_ref[group, ghost, :]
            grid_ref[pl.ds(pl.multiple_of(k * grid_n + mine, len_y), 8), :] += got_ref[group, ghost, :]
        size = len(planes) * grid_n
        half = grid_n // 2
        mid_ref[pl.ds(0, size), :] = dot3(split_bf16(grid_ref[pl.ds(0, size), :]), (tx_ref[0], tx_ref[1]))
        columns = [jnp.concatenate([mid_ref[pl.ds(k * grid_n, grid_n), pl.ds(c * half, half)] for c in range(2)], axis=0) for k in range(len(planes))]
        modes = dot3((ty_ref[0], ty_ref[1]), split_bf16(jnp.concatenate(columns, axis=1)))
        grid_ref[:, pl.ds(0, len(planes) * half)] = modes
        peak = jnp.maximum(jnp.max(jnp.abs(modes), keepdims=True), 1e-30)
        parts = [(grid_ref[:, pl.ds(k * half, half)] * (CODE_MAX / peak)).reshape(z_devs, 8, half) for k in range(len(planes))]
        if len(planes) == 1:
            parts.append(jnp.zeros((z_devs, 8, half), F32))
        codes = jnp.round(jnp.concatenate(parts, axis=1)).astype(jnp.int32).astype(jnp.int16)
        code_ref[group] = codes
        scale_ref[group] = jnp.broadcast_to(peak * (1.0 / CODE_MAX), (8, 128))

        @pl.loop(1, z_devs)
        def _(step):
            for copy in send(group, step):
                copy.start()

        recv_ref[group, my_z] = code_ref[group, my_z]
        rscale_ref[group, my_z, pl.ds(0, 1)] = scale_ref[group, pl.ds(0, 1)]

    def decode(group):
        pltpu.make_async_copy(recv_ref.at[group, pl.ds(0, z_devs - 1)], recv_ref.at[group, pl.ds(0, z_devs - 1)], recv_sem.at[group]).wait()
        pltpu.make_async_copy(rscale_ref.at[group, pl.ds(0, z_devs - 1), pl.ds(0, 1)], rscale_ref.at[group, pl.ds(0, z_devs - 1), pl.ds(0, 1)], srecv_sem.at[group]).wait()
        return recv_ref[group].astype(jnp.int32).astype(F32) * rscale_ref[group, :, pl.ds(0, 1), :]

    def transform_z(part):
        flat = deq_ref.at[part]
        columns = [flat[pl.ds(ky, grid_n, stride=4), :] for ky in range(4)]
        zed = dot3((tz_ref[part, 0], tz_ref[part, 1]), split_bf16(jnp.concatenate(columns, axis=1)))
        if part == 0:
            zed_ref[...] = zed
        else:
            zed_ref[...] += zed

    acc_ref[...] = jnp.zeros_like(acc_ref)
    for group in range(n_groups):
        @pl.loop(0, slots // CHUNK)
        def _(i):
            spread(group, i * CHUNK)
            if group:
                @pl.when(i == STEP_AT)
                def _():
                    transform_send(group - 1)

        if group == 0:
            pl.semaphore_wait(barrier, z_devs)
            for load in loads:
                load.wait()
        swap(group).start()
    transform_send(n_groups - 1)

    rows = z_devs * 16
    first = decode(0)
    late = decode(2)
    deq_ref[0] = first.reshape(rows, 128)
    deq_ref[0, pl.ds(16, rows - 16), :] += late[:z_devs - 1].reshape(rows - 16, 128)
    deq_ref[0, pl.ds(0, 16), :] += late[z_devs - 1]
    transform_z(0)
    deq_ref[1] = decode(1).reshape(rows, 128)
    late = decode(3)
    deq_ref[1, pl.ds(16, rows - 16), :] += late[:z_devs - 1].reshape(rows - 16, 128)
    deq_ref[1, pl.ds(0, 16), :] += late[z_devs - 1]
    transform_z(1)

    half = grid_n // 2
    row = jnp.zeros((8, grid_n), F32)
    for ky in range(4):
        cols = pl.ds(ky * half, half)
        real, imag = zed_ref[pl.ds(0, grid_n), cols], zed_ref[pl.ds(grid_n, grid_n), cols]
        value = 0.5 * bc_ref[:, ky, :] * (real * real + imag * imag).T
        ek_ref[:, ky, :] = value
        row += jnp.sum(value.reshape(half // 8, 8, grid_n), axis=0)
    store = pltpu.make_async_copy(ek_ref, ek_hbm, load_sem.at[0])
    store.start()
    row_ref[0] = jnp.broadcast_to(jnp.sum(row[:, :half] + row[:, half:], axis=0, keepdims=True), (8, half))

    def pair_copy():
        return pltpu.make_async_remote_copy(src_ref=row_ref.at[0], dst_ref=row_ref.at[1], send_sem=row_sem.at[0], recv_sem=row_sem.at[1], device_id=partner, device_id_type=MESH)

    def row_copy(step):
        return pltpu.make_async_remote_copy(src_ref=row_ref.at[2, pl.ds(0, 1)], dst_ref=rrow_ref.at[my_z, pl.ds(0, 1)], send_sem=row_sem.at[2], recv_sem=row_sem.at[3], device_id={'zdom': chip(step)}, device_id_type=MESH)

    pair_copy().start()
    pair_copy().wait()
    row_ref[2] = row_ref[0] + row_ref[1]

    @pl.loop(1, z_devs)
    def _(step):
        row_copy(step).start()

    rrow_ref[my_z, pl.ds(0, 1)] = row_ref[2, pl.ds(0, 1)]
    others = rrow_ref.at[pl.ds(0, z_devs - 1), pl.ds(0, 1)]
    pltpu.make_async_copy(others, others, row_sem.at[3]).wait()
    sum_ref[0] = jnp.sum(rrow_ref[:, pl.ds(0, 1), :]) * (1.0 / (grid_n * grid_n * grid_n))
    pltpu.make_async_copy(others, others, row_sem.at[2]).wait()
    for group in range(n_groups):
        sent = code_ref.at[group, pl.ds(0, z_devs - 1)]
        pltpu.make_async_copy(sent, sent, send_sem.at[group]).wait()
        sent = rscale_ref.at[group, pl.ds(0, z_devs - 1), pl.ds(0, 1)]
        pltpu.make_async_copy(sent, sent, ssend_sem.at[group]).wait()
    store.wait()


def solution(mesh):
    y_devs = mesh.shape['ydom']
    z_devs = mesh.shape['zdom']
    slot_spec = P(('sys', 'ydom', 'zdom'))
    mode_spec = P(('sys', 'ydom'), 'zdom', None)

    def local_energy(charge, real_mask, grid_idx, spline_w, influence):
        grid_n = influence.shape[2]
        slots = charge.shape[0]
        half = grid_n // 2
        n_groups = len(GROUPS)
        table_x, table_y, table_z = dft_tables(grid_n, y_devs, z_devs)
        any_spec = pl.BlockSpec(memory_space=pl.ANY)
        vmem_spec = pl.BlockSpec(memory_space=pltpu.VMEM)
        rows = grid_n + 16
        mode_energy, energy = pl.pallas_call(
            functools.partial(energy_kernel, y_devs, z_devs),
            in_specs=[vmem_spec] * 4 + [any_spec] * 4,
            out_specs=[any_spec, pl.BlockSpec(memory_space=pltpu.SMEM)],
            out_shape=[jax.ShapeDtypeStruct(influence.shape, F32), jax.ShapeDtypeStruct((1,), F32)],
            scratch_shapes=[
                pltpu.VMEM((slots, grid_n), BF16), pltpu.VMEM((slots, grid_n), BF16),
                pltpu.VMEM((2, rows, SUB), BF16), pltpu.VMEM((2, rows, SUB), BF16),
                pltpu.VMEM((n_groups, rows, grid_n), F32), pltpu.VMEM((n_groups, rows, grid_n), F32),
                pltpu.VMEM((2 * grid_n, grid_n), F32), pltpu.VMEM((2 * grid_n, grid_n), F32),
                pltpu.VMEM((n_groups, z_devs, 16, half), jnp.int16), pltpu.VMEM((n_groups, z_devs, 16, half), jnp.int16),
                pltpu.VMEM((n_groups, 8, 128), F32), pltpu.VMEM((n_groups, z_devs, 8, 128), F32),
                pltpu.VMEM((2, z_devs * 16, half), F32), pltpu.VMEM((2 * grid_n, 4 * half), F32),
                pltpu.VMEM(influence.shape, F32), pltpu.VMEM(influence.shape, F32),
                pltpu.VMEM(table_x.shape[1:], BF16), pltpu.VMEM(table_y.shape, BF16), pltpu.VMEM(table_z.shape, BF16),
                pltpu.VMEM((3, 8, 128), F32), pltpu.VMEM((z_devs, 8, 128), F32),
                pltpu.SemaphoreType.DMA((4,)), pltpu.SemaphoreType.DMA((2, n_groups)),
                pltpu.SemaphoreType.DMA((n_groups,)), pltpu.SemaphoreType.DMA((n_groups,)),
                pltpu.SemaphoreType.DMA((n_groups,)), pltpu.SemaphoreType.DMA((n_groups,)),
                pltpu.SemaphoreType.DMA((4,)),
            ],
            compiler_params=pltpu.CompilerParams(collective_id=0, has_side_effects=True, vmem_limit_bytes=60 * 1024 * 1024),
            name="energy",
        )(charge.reshape(1, slots), real_mask.reshape(1, slots), grid_idx.T, jnp.transpose(spline_w, (1, 2, 0)), influence, jnp.asarray(table_x), jnp.asarray(table_y), jnp.asarray(table_z))
        return mode_energy, energy

    return jax.shard_map(local_energy, mesh=mesh, in_specs=(slot_spec, slot_spec, P(('sys', 'ydom', 'zdom'), None), P(('sys', 'ydom', 'zdom'), None, None), mode_spec), out_specs=(mode_spec, P('sys')), check_vma=False)
```

time: 265 us -> 89.7 us (0.34)
  blocking collectives: 91.1 us -> 0 us
  Pallas kernels: 0 us -> 85.3 us
  other arithmetic: 83.8 us -> 0 us
  matrix products: 61.3 us -> 0 us
  waiting for transfers between devices: 15 us -> 0 us
  local copies, waits for them, and re-layouts: 7.8 us -> 1.87 us
  starting transfers between devices: 3.05 us -> 0 us
    pallas_call x0 -> x1, Pallas kernels: none -> 85.3 us  [local_energy(): pl.pallas_call(functools.partial(energy_kernel, y_devs, z_devs), in_specs...]
    psum x1 -> x0, blocking collectives: 62.2 us -> none  [local_energy(): lax.psum(jnp.sum(mode_energy), ('ydom', 'zdom'))]
    dot_general x4 -> x0, matrix products: 61.3 us -> none  [the longest x1 54.9 us: spread_block(): jnp.einsum('...nx,...nyz->...xyz', line_x, plane_yz, precision=PRECISE, p...]
    reduce_sum x4 -> x0, other arithmetic: 58.1 us -> none  [the longest x3 56.3 us: tap_weights(): return jnp.sum(jnp.where(hit_mask, taps_w[..., None, :], 0.0), axis=-1)]
    all_to_all x2 -> x0, blocking collectives: 28.9 us -> none  [the longest x1 23.3 us: local_energy(): stage_y = lax.all_to_all(stage_y, 'zdom', 2, 3, tiled=True)]
    dot_general x1 -> x0, other arithmetic: 22.7 us -> none  [spread_block(): jnp.einsum('...nx,...nyz->...xyz', line_x, plane_yz, precision=PRECISE, p...]
    ppermute x2 -> x0, waiting for transfers between devices: 15 us -> none  [fold_ghosts(): lax.ppermute(ghost_slab, axis_name, [(source, (source + 1) % axis_size) f...]
    ppermute x2 -> x0, starting transfers between devices: 3.05 us -> none  [fold_ghosts(): lax.ppermute(ghost_slab, axis_name, [(source, (source + 1) % axis_size) f...]
  transfers between devices with their start and end apart: 2 -> 0, of which waited for: 2 -> 0; matrix products, arithmetic and copies ran while one was open for 1% -> 0% of each run, Pallas kernels for 0% -> 0%
where the time goes in v2:
time: 89.7 us; the launch traced here: 89.5 us
  Pallas kernels  85.3 us (95%)
  between operations  2.34 us (3%)
  local copies, waits for them, and re-layouts  1.87 us (2%)
    pallas_call x1, Pallas kernels, local_energy(): pl.pallas_call(functools.partial(energy_kernel, y_devs, z_devs), in_specs...  85.3 us
    unnamed x1, local copies, waits for them, and re-layouts  1.87 us

profile of v2, /device:TPU:1, one launch (start us, length us, event | category | flops | bytes accessed | tf_op | source)
XLA Modules:
  0.0 89.5 jit_solution(16225846914394813552)
XLA Ops:
  0.6 85.3 %energy.1 = (f32[128,4,256]{2,1,0:T(4,128)}, f32[1]{0:T(128)}) custom-call(f32[1,16384]{1,0:T(1,128)} %bitcast.6, s32[1,16384]{1,0:T(1,128)} %bitcast.7, s32[3,16384]{1,0:T(4,128)} %bitcast.5, f32[3,4,16384]{2,1,0:T(4,128)} %bitcast.4, f32[128,4,256]{2,1,0:T(4,128)} %bc_hbm.1, bf16[2,2,256,256]{3,2,1,0:T(8,128)(2,1)} %constant.6.clone.tx_hbm, ...), custom_call_target="tpu_custom_call" | custom-call | tf_op jit(solution)/shard_map/energy/pallas_call | solution.py:276
  85.9 1.9 %copy.12 = f32[128,4,256]{2,1,0:T(4,128)} copy(f32[128,4,256]{2,1,0:T(4,128)} %get-tuple-element.4) | data formatting | bytes 1048576

commit v3 on v2

v3 whole, which is shorter than its diff:
```python
import functools
import math
import jax
import jax.numpy as jnp
import numpy as np
from jax import lax
from jax.experimental import pallas as pl
from jax.experimental.pallas import tpu as pltpu
from jax.sharding import PartitionSpec as P

F32 = jnp.float32
BF16 = jnp.bfloat16
SUB = 256
CHUNK = 1024
GROUPS = ((0, 1, 2, 3), (4, 5), (6,))
STEP_AT = (0, 5, 7)
EARLY = 2048
CODE_MAX = 32767.0
MESH = pl.DeviceIdType.MESH


def split_bf16(value):
    high = value.astype(BF16)
    return high, (value - high.astype(F32)).astype(BF16)


def dot3(lhs, rhs):
    def dot(a, b):
        return jnp.dot(a, b, preferred_element_type=F32)
    return dot(lhs[0], rhs[0]) + dot(lhs[1], rhs[0]) + dot(lhs[0], rhs[1])


def np_split(value):
    value = np.asarray(value, np.float32)
    high = value.astype(BF16)
    return np.stack([high, (value - high.astype(np.float32)).astype(BF16)])


def dft_tables(grid_n, y_devs, z_devs):
    turn = 2.0 * np.pi / grid_n
    len_y, len_z = grid_n // y_devs, grid_n // z_devs
    x = np.arange(grid_n)
    freq = np.arange(grid_n)
    phase_x = (np.outer(x, freq) % grid_n) * turn
    table_x = np.stack([np_split(np.concatenate([np.cos(phase_x[:, i * len_y:(i + 1) * len_y]), -np.sin(phase_x[:, i * len_y:(i + 1) * len_y])], axis=1)) for i in range(y_devs)])
    phase_y = (np.outer(freq, x) % grid_n) * turn
    real = np.concatenate([np.cos(phase_y), np.sin(phase_y)], axis=1)
    imag = np.concatenate([-np.sin(phase_y), np.cos(phase_y)], axis=1)
    rows = np.stack([real.reshape(z_devs, len_z, 2 * grid_n), imag.reshape(z_devs, len_z, 2 * grid_n)], axis=1)
    table_y = np_split(rows.reshape(2 * grid_n, 2 * grid_n))
    table_z = []
    for first in (0, 2):
        pos = np.arange(z_devs)[:, None] * len_z + first + np.arange(2)[None, :]
        phase_z = ((freq[:, None, None] * pos[None]) % grid_n) * turn
        real = np.stack([np.cos(phase_z), np.sin(phase_z)], axis=3).reshape(grid_n, -1)
        imag = np.stack([-np.sin(phase_z), np.cos(phase_z)], axis=3).reshape(grid_n, -1)
        table_z.append(np_split(np.concatenate([real, imag], axis=0)))
    return table_x, table_y, np.stack(table_z)


def ghost_rows(group):
    return -(-8 * len(GROUPS[group]) // 16) * 16


def energy_kernel(y_devs, z_devs, q_hbm, m_hbm, idx_hbm, w_hbm, bc_hbm, tx_hbm, ty_hbm, tz_hbm, ek_hbm, sum_ref,
                  q_ref, m_ref, idx_ref, w_ref, line_ref, xh_ref, xl_ref, ph_ref, pl_ref, acc_refs, got_refs, grid_ref, mid_ref, mode_ref,
                  code_refs, recv_refs, scale_ref, rscale_ref,
                  deq_ref, zed_ref, bc_ref, ek_ref, tx_ref, ty_ref, tz_ref, row_ref, rrow_ref,
                  early_sem, load_sem, swap_sem, send_sem, recv_sem, ssend_sem, srecv_sem, row_sem):
    my_y = lax.axis_index('ydom')
    my_z = lax.axis_index('zdom')
    grid_n = xh_ref.shape[1]
    slots = q_ref.shape[1]
    len_y = grid_n // y_devs
    half = grid_n // 2
    n_groups = len(GROUPS)
    barrier = pltpu.get_barrier_semaphore()
    partner = {'ydom': 1 - my_y}

    def chip(step):
        return (my_z + step) & (z_devs - 1)

    def slot_loads(piece):
        cols = pl.ds(0, EARLY) if piece == 0 else pl.ds(EARLY, slots - EARLY)
        return [pltpu.make_async_copy(hbm.at[lead + (cols,)], ref.at[lead + (cols,)], early_sem.at[piece, k])
                for k, (hbm, ref, lead) in enumerate(((q_hbm, q_ref, (slice(None),)), (m_hbm, m_ref, (slice(None),)), (idx_hbm, idx_ref, (slice(None),)), (w_hbm, w_ref, (slice(None), slice(None)))))]

    for piece in range(2):
        for load in slot_loads(piece):
            load.start()

    @pl.loop(1, z_devs)
    def _(step):
        pl.semaphore_signal(barrier, inc=1, device_id={'zdom': chip(step)}, device_id_type=MESH)

    pl.semaphore_signal(barrier, inc=1, device_id=partner, device_id_type=MESH)

    loads = [pltpu.make_async_copy(tx_hbm.at[my_y], tx_ref, load_sem.at[0]), pltpu.make_async_copy(ty_hbm, ty_ref, load_sem.at[1]),
             pltpu.make_async_copy(tz_hbm, tz_ref, load_sem.at[2]), pltpu.make_async_copy(bc_hbm, bc_ref, load_sem.at[3])]
    for load in loads:
        load.start()

    def swap(group):
        return pltpu.make_async_remote_copy(src_ref=acc_refs[group], dst_ref=got_refs[group], send_sem=swap_sem.at[0, group], recv_sem=swap_sem.at[1, group], device_id=partner, device_id_type=MESH)

    def send(group, step):
        other = chip(step)
        return pltpu.make_async_remote_copy(src_ref=code_refs[group].at[other], dst_ref=recv_refs[group].at[my_z], send_sem=send_sem.at[group], recv_sem=recv_sem.at[group], device_id={'zdom': other}, device_id_type=MESH)

    def send_scale(last, step):
        return pltpu.make_async_remote_copy(src_ref=scale_ref.at[last, pl.ds(0, 2 - last)], dst_ref=rscale_ref.at[last, my_z, pl.ds(0, 2 - last)], send_sem=ssend_sem.at[last], recv_sem=srecv_sem.at[last], device_id={'zdom': chip(step)}, device_id_type=MESH)

    def spread(group, base):
        planes = GROUPS[group]
        total = None
        for sub in range(CHUNK // SUB):
            slot = sub % 2
            cols = pl.ds(pl.multiple_of(base + sub * SUB, SUB), SUB)
            if group == 0:
                tap = lax.broadcasted_iota(jnp.int32, (4, SUB), 0)
                weight = q_ref[:, cols] * m_ref[:, cols].astype(F32)
                pos_x = ((idx_ref[0:1, cols] + tap) & (grid_n - 1)).astype(F32).astype(BF16)
                wxh, wxl = split_bf16(w_ref[0, :, cols] * weight)
                row_x = lax.broadcasted_iota(jnp.int32, (grid_n, SUB), 0).astype(F32).astype(BF16)
                line_h = jnp.zeros((grid_n, SUB), BF16)
                line_l = jnp.zeros((grid_n, SUB), BF16)
                for s in range(4):
                    hit = row_x == pos_x[s:s + 1]
                    line_h = jnp.where(hit, wxh[s:s + 1], line_h)
                    line_l = jnp.where(hit, wxl[s:s + 1], line_l)
                xh_ref[cols, :] = line_h.T
                xl_ref[cols, :] = line_l.T
                pos_y = idx_ref[1:2, cols] + tap
                pos_z = idx_ref[2:3, cols] + tap
                wy = w_ref[1, :, cols]
                wz = w_ref[2, :, cols]
                row_8 = lax.broadcasted_iota(jnp.int32, (8, SUB), 0)
                line_z = jnp.zeros((8, SUB), F32)
                ghost_y = jnp.zeros((8, SUB), F32)
                row_y = lax.broadcasted_iota(jnp.int32, (len_y, SUB), 0)
                line_y = jnp.zeros((len_y, SUB), F32)
                for t in range(4):
                    line_z = jnp.where(row_8 == pos_z[t:t + 1], wz[t:t + 1], line_z)
                    ghost_y = jnp.where(row_8 + len_y == pos_y[t:t + 1], wy[t:t + 1], ghost_y)
                    line_y = jnp.where(row_y == pos_y[t:t + 1], wy[t:t + 1], line_y)
                line_ref[pl.ds(0, len_y), cols] = line_y
                line_ref[pl.ds(len_y, 8), cols] = ghost_y
                line_ref[pl.ds(len_y + 8, 8), cols] = line_z
            else:
                line_y = line_ref[pl.ds(0, len_y), cols]
                ghost_y = line_ref[pl.ds(len_y, 8), cols]
                line_z = line_ref[pl.ds(len_y + 8, 8), cols]
            for k, z in enumerate(planes):
                high, low = split_bf16(line_y * line_z[z:z + 1])
                ph_ref[slot, k * len_y:(k + 1) * len_y, :] = high
                pl_ref[slot, k * len_y:(k + 1) * len_y, :] = low
            ghosts = [ghost_y * line_z[z:z + 1] for z in planes]
            if len(planes) % 2:
                ghosts.append(jnp.zeros((8, SUB), F32))
            high, low = split_bf16(jnp.concatenate(ghosts, axis=0))
            top = len(planes) * len_y
            rows = pl.ds(0, top + ghost_rows(group))
            ph_ref[slot, top:top + ghost_rows(group), :] = high
            pl_ref[slot, top:top + ghost_rows(group), :] = low
            part = dot3((ph_ref[slot, rows, :], pl_ref[slot, rows, :]), (xh_ref[cols, :], xl_ref[cols, :]))
            total = part if total is None else total + part
        acc_refs[group][...] += total

    def transform_send(group):
        planes = GROUPS[group]
        acc_ref, got_ref = acc_refs[group], got_refs[group]
        swap(group).wait()
        mine, theirs = my_y * len_y, (1 - my_y) * len_y
        peak = jnp.full((1, 1), 1e-30, F32)
        for first in range(0, len(planes), 2):
            count = min(2, len(planes) - first)
            for k in range(count):
                block = pl.ds((first + k) * len_y, len_y)
                grid_ref[pl.ds(pl.multiple_of(k * grid_n + mine, len_y), len_y), :] = acc_ref[block, :]
                grid_ref[pl.ds(pl.multiple_of(k * grid_n + theirs, len_y), len_y), :] = got_ref[block, :]
            for k in range(count):
                ghost = pl.ds(len(planes) * len_y + 8 * (first + k), 8)
                grid_ref[pl.ds(pl.multiple_of(k * grid_n + theirs, len_y), 8), :] += acc_ref[ghost, :]
                grid_ref[pl.ds(pl.multiple_of(k * grid_n + mine, len_y), 8), :] += got_ref[ghost, :]
            size = count * grid_n
            mid_ref[pl.ds(0, size), :] = dot3(split_bf16(grid_ref[pl.ds(0, size), :]), (tx_ref[0], tx_ref[1]))
            columns = [jnp.concatenate([mid_ref[pl.ds(k * grid_n, grid_n), pl.ds(c * half, half)] for c in range(2)], axis=0) for k in range(count)]
            modes = dot3((ty_ref[0], ty_ref[1]), split_bf16(jnp.concatenate(columns, axis=1)))
            mode_ref[:, pl.ds(first * half, count * half)] = modes
            peak = jnp.maximum(peak, jnp.max(jnp.abs(modes), keepdims=True))
        gain = CODE_MAX / peak
        for k in range(len(planes)):
            codes = jnp.round(mode_ref[:, pl.ds(k * half, half)] * gain).astype(jnp.int32).astype(jnp.int16)
            code_refs[group][:, k] = codes.reshape(z_devs, 8, half)
        last = group // 2
        scale_ref[last, pl.ds(group % 2, 1)] = jnp.broadcast_to(peak * (1.0 / CODE_MAX), (1, 128))

        @pl.loop(1, z_devs)
        def _(step):
            send(group, step).start()
            if group:
                send_scale(last, step).start()

        recv_refs[group][my_z] = code_refs[group][my_z]
        if group:
            rscale_ref[last, my_z] = scale_ref[last]

    def await_all(ref, sem):
        pltpu.make_async_copy(ref, ref, sem).wait()

    def await_codes(group):
        await_all(recv_refs[group].at[pl.ds(0, z_devs - 1)], recv_sem.at[group])

    def await_scale(last):
        await_all(rscale_ref.at[last, pl.ds(0, z_devs - 1), pl.ds(0, 2 - last)], srecv_sem.at[last])

    def decode(group, planes):
        codes = recv_refs[group][:, planes].astype(jnp.int32).astype(F32)
        return codes * rscale_ref[group // 2, :, pl.ds(group % 2, 1), :].reshape(z_devs, 1, 1, half)

    def fold(part, planes):
        rows = z_devs * 16
        flat = planes.reshape(rows, half)
        deq_ref[part, pl.ds(16, rows - 16), :] += flat[:rows - 16]
        deq_ref[part, pl.ds(0, 16), :] += flat[rows - 16:]

    def transform_z(part):
        flat = deq_ref.at[part]
        columns = [flat[pl.ds(ky, grid_n, stride=4), :] for ky in range(4)]
        zed = dot3((tz_ref[part, 0], tz_ref[part, 1]), split_bf16(jnp.concatenate(columns, axis=1)))
        if part == 0:
            zed_ref[...] = zed
        else:
            zed_ref[...] += zed

    for acc_ref in acc_refs:
        acc_ref[...] = jnp.zeros_like(acc_ref)
    for load in slot_loads(0):
        load.wait()
    for group in range(n_groups):
        @pl.loop(0, slots // CHUNK)
        def _(i):
            if group == 0:
                @pl.when(i == EARLY // CHUNK)
                def _():
                    for load in slot_loads(1):
                        load.wait()

            spread(group, i * CHUNK)
            if group:
                @pl.when(i == STEP_AT[group])
                def _():
                    transform_send(group - 1)

        if group == 0:
            pl.semaphore_wait(barrier, z_devs)
            for load in loads:
                load.wait()
        swap(group).start()
    transform_send(n_groups - 1)

    rows = z_devs * 16
    await_codes(0)
    await_scale(0)
    for part in range(2):
        deq_ref[part] = decode(0, slice(2 * part, 2 * part + 2)).reshape(rows, half)
    await_codes(1)
    fold(0, decode(1, slice(0, 2)))
    transform_z(0)
    await_codes(2)
    await_scale(1)
    late = decode(2, slice(0, 1))
    fold(1, jnp.concatenate([late, jnp.zeros_like(late)], axis=1))
    transform_z(1)

    row = jnp.zeros((8, grid_n), F32)
    for ky in range(4):
        cols = pl.ds(ky * half, half)
        real, imag = zed_ref[pl.ds(0, grid_n), cols], zed_ref[pl.ds(grid_n, grid_n), cols]
        value = 0.5 * bc_ref[:, ky, :] * (real * real + imag * imag).T
        ek_ref[:, ky, :] = value
        row += jnp.sum(value.reshape(half // 8, 8, grid_n), axis=0)
    store = pltpu.make_async_copy(ek_ref, ek_hbm, load_sem.at[0])
    store.start()
    row_ref[0] = jnp.broadcast_to(jnp.sum(row[:, :half] + row[:, half:], axis=0, keepdims=True), (8, half))

    def pair_copy():
        return pltpu.make_async_remote_copy(src_ref=row_ref.at[0], dst_ref=row_ref.at[1], send_sem=row_sem.at[0], recv_sem=row_sem.at[1], device_id=partner, device_id_type=MESH)

    def row_copy(step):
        return pltpu.make_async_remote_copy(src_ref=row_ref.at[2, pl.ds(0, 1)], dst_ref=rrow_ref.at[my_z, pl.ds(0, 1)], send_sem=row_sem.at[2], recv_sem=row_sem.at[3], device_id={'zdom': chip(step)}, device_id_type=MESH)

    pair_copy().start()
    pair_copy().wait()
    row_ref[2] = row_ref[0] + row_ref[1]

    @pl.loop(1, z_devs)
    def _(step):
        row_copy(step).start()

    rrow_ref[my_z, pl.ds(0, 1)] = row_ref[2, pl.ds(0, 1)]
    others = rrow_ref.at[pl.ds(0, z_devs - 1), pl.ds(0, 1)]
    pltpu.make_async_copy(others, others, row_sem.at[3]).wait()
    sum_ref[0] = jnp.sum(rrow_ref[:, pl.ds(0, 1), :]) * (1.0 / (grid_n * grid_n * grid_n))
    await_all(others, row_sem.at[2])
    for group in range(n_groups):
        await_all(code_refs[group].at[pl.ds(0, z_devs - 1)], send_sem.at[group])
    for last in range(2):
        await_all(rscale_ref.at[last, pl.ds(0, z_devs - 1), pl.ds(0, 2 - last)], ssend_sem.at[last])
    store.wait()


def solution(mesh):
    y_devs = mesh.shape['ydom']
    z_devs = mesh.shape['zdom']
    slot_spec = P(('sys', 'ydom', 'zdom'))
    mode_spec = P(('sys', 'ydom'), 'zdom', None)

    def local_energy(charge, real_mask, grid_idx, spline_w, influence):
        grid_n = influence.shape[2]
        slots = charge.shape[0]
        half = grid_n // 2
        n_groups = len(GROUPS)
        table_x, table_y, table_z = dft_tables(grid_n, y_devs, z_devs)
        any_spec = pl.BlockSpec(memory_space=pl.ANY)
        rows = [len(GROUPS[g]) * (grid_n // y_devs) + ghost_rows(g) for g in range(n_groups)]
        codes = [pltpu.VMEM((z_devs, len(planes), 8, half), jnp.int16) for planes in GROUPS]
        mode_energy, energy = pl.pallas_call(
            functools.partial(energy_kernel, y_devs, z_devs),
            in_specs=[any_spec] * 8,
            out_specs=[any_spec, pl.BlockSpec(memory_space=pltpu.SMEM)],
            out_shape=[jax.ShapeDtypeStruct(influence.shape, F32), jax.ShapeDtypeStruct((1,), F32)],
            scratch_shapes=[
                pltpu.VMEM((1, slots), F32), pltpu.VMEM((1, slots), jnp.int32), pltpu.VMEM((3, slots), jnp.int32), pltpu.VMEM((3, 4, slots), F32),
                pltpu.VMEM((grid_n // y_devs + 16, slots), F32),
                pltpu.VMEM((slots, grid_n), BF16), pltpu.VMEM((slots, grid_n), BF16),
                pltpu.VMEM((2, rows[0], SUB), BF16), pltpu.VMEM((2, rows[0], SUB), BF16),
                [pltpu.VMEM((r, grid_n), F32) for r in rows], [pltpu.VMEM((r, grid_n), F32) for r in rows],
                pltpu.VMEM((2 * grid_n, grid_n), F32), pltpu.VMEM((2 * grid_n, grid_n), F32), pltpu.VMEM((2 * grid_n, 4 * half), F32),
                codes, codes,
                pltpu.VMEM((2, 2, 128), F32), pltpu.VMEM((2, z_devs, 2, 128), F32),
                pltpu.VMEM((2, z_devs * 16, half), F32), pltpu.VMEM((2 * grid_n, 4 * half), F32),
                pltpu.VMEM(influence.shape, F32), pltpu.VMEM(influence.shape, F32),
                pltpu.VMEM(table_x.shape[1:], BF16), pltpu.VMEM(table_y.shape, BF16), pltpu.VMEM(table_z.shape, BF16),
                pltpu.VMEM((3, 8, 128), F32), pltpu.VMEM((z_devs, 8, 128), F32),
                pltpu.SemaphoreType.DMA((2, 4)), pltpu.SemaphoreType.DMA((4,)), pltpu.SemaphoreType.DMA((2, n_groups)),
                pltpu.SemaphoreType.DMA((n_groups,)), pltpu.SemaphoreType.DMA((n_groups,)),
                pltpu.SemaphoreType.DMA((2,)), pltpu.SemaphoreType.DMA((2,)),
                pltpu.SemaphoreType.DMA((4,)),
            ],
            compiler_params=pltpu.CompilerParams(collective_id=0, has_side_effects=True, vmem_limit_bytes=60 * 1024 * 1024),
            name="energy",
        )(charge.reshape(1, slots), real_mask.reshape(1, slots), grid_idx.T, jnp.transpose(spline_w, (1, 2, 0)), influence, jnp.asarray(table_x), jnp.asarray(table_y), jnp.asarray(table_z))
        return mode_energy, energy

    return jax.shard_map(local_energy, mesh=mesh, in_specs=(slot_spec, slot_spec, P(('sys', 'ydom', 'zdom'), None), P(('sys', 'ydom', 'zdom'), None, None), mode_spec), out_specs=(mode_spec, P('sys')), check_vma=False)
```

time: 89.7 us -> 76.2 us (0.85)
  Pallas kernels: 85.3 us -> 71.8 us
    pallas_call x1, Pallas kernels: 85.3 us -> 71.8 us  [local_energy(): pl.pallas_call(functools.partial(energy_kernel, y_devs, z_devs), in_specs...]
where the time goes in v3:
time: 76.2 us; the launch traced here: 76 us
  Pallas kernels  71.8 us (94%)
  between operations  2.34 us (3%)
  local copies, waits for them, and re-layouts  1.87 us (2%)
    pallas_call x1, Pallas kernels, local_energy(): pl.pallas_call(functools.partial(energy_kernel, y_devs, z_devs), in_specs...  71.8 us
    unnamed x1, local copies, waits for them, and re-layouts  1.87 us

profile of v3, /device:TPU:1, one launch (start us, length us, event | category | flops | bytes accessed | tf_op | source)
XLA Modules:
  0.0 76.0 jit_solution(3502167538017218932)
XLA Ops:
  0.6 71.8 %energy.1 = (f32[128,4,256]{2,1,0:T(4,128)}, f32[1]{0:T(128)}) custom-call(f32[1,16384]{1,0:T(1,128)} %bitcast.6, s32[1,16384]{1,0:T(1,128)} %bitcast.7, s32[3,16384]{1,0:T(4,128)} %bitcast.5, f32[3,4,16384]{2,1,0:T(4,128)} %bitcast.4, f32[128,4,256]{2,1,0:T(4,128)} %bc_hbm.1, bf16[2,2,256,256]{3,2,1,0:T(8,128)(2,1)} %constant.6.clone.tx_hbm, ...), custom_call_target="tpu_custom_call" | custom-call | tf_op jit(solution)/shard_map/energy/pallas_call | solution.py:328
  72.4 1.9 %copy.12 = f32[128,4,256]{2,1,0:T(4,128)} copy(f32[128,4,256]{2,1,0:T(4,128)} %get-tuple-element.4) | data formatting | bytes 1048576

commit v4 on v3

--- a/solution.py
+++ b/solution.py
@@ -24,10 +24,18 @@
     return high, (value - high.astype(F32)).astype(BF16)
 
 
-def dot3(lhs, rhs):
+def dot3(lhs, rhs, rhs_dim=0):
     def dot(a, b):
-        return jnp.dot(a, b, preferred_element_type=F32)
+        return lax.dot_general(a, b, (((1,), (rhs_dim,)), ((), ())), preferred_element_type=F32)
     return dot(lhs[0], rhs[0]) + dot(lhs[1], rhs[0]) + dot(lhs[0], rhs[1])
+
+
+def pick(ahead, taps, wrap=True):
+    place = ahead & 15 if wrap else ahead
+    value = jnp.zeros(ahead.shape, F32)
+    for t in range(4):
+        value = jnp.where(place == t, taps[t:t + 1], value)
+    return value
 
 
 def np_split(value):
@@ -63,7 +71,7 @@
 
 
 def energy_kernel(y_devs, z_devs, q_hbm, m_hbm, idx_hbm, w_hbm, bc_hbm, tx_hbm, ty_hbm, tz_hbm, ek_hbm, sum_ref,
-                  q_ref, m_ref, idx_ref, w_ref, line_ref, xh_ref, xl_ref, ph_ref, pl_ref, acc_refs, got_refs, grid_ref, mid_ref, mode_ref,
+                  q_ref, m_ref, idx_ref, w_ref, near_ref, xh_ref, xl_ref, ph_ref, pl_ref, acc_refs, got_refs, grid_ref, mid_ref, mode_ref,
                   code_refs, recv_refs, scale_ref, rscale_ref,
                   deq_ref, zed_ref, bc_ref, ek_ref, tx_ref, ty_ref, tz_ref, row_ref, rrow_ref,
                   early_sem, load_sem, swap_sem, send_sem, recv_sem, ssend_sem, srecv_sem, row_sem):
@@ -112,48 +120,37 @@
 
     def spread(group, base):
         planes = GROUPS[group]
+        zero_16 = jnp.zeros((16, SUB), BF16)
         total = None
         for sub in range(CHUNK // SUB):
             slot = sub % 2
             cols = pl.ds(pl.multiple_of(base + sub * SUB, SUB), SUB)
+            row_16 = lax.broadcasted_iota(jnp.int32, (16, SUB), 0)
             if group == 0:
-                tap = lax.broadcasted_iota(jnp.int32, (4, SUB), 0)
                 weight = q_ref[:, cols] * m_ref[:, cols].astype(F32)
-                pos_x = ((idx_ref[0:1, cols] + tap) & (grid_n - 1)).astype(F32).astype(BF16)
-                wxh, wxl = split_bf16(w_ref[0, :, cols] * weight)
-                row_x = lax.broadcasted_iota(jnp.int32, (grid_n, SUB), 0).astype(F32).astype(BF16)
-                line_h = jnp.zeros((grid_n, SUB), BF16)
-                line_l = jnp.zeros((grid_n, SUB), BF16)
-                for s in range(4):
-                    hit = row_x == pos_x[s:s + 1]
-                    line_h = jnp.where(hit, wxh[s:s + 1], line_h)
-                    line_l = jnp.where(hit, wxl[s:s + 1], line_l)
-                xh_ref[cols, :] = line_h.T
-                xl_ref[cols, :] = line_l.T
-                pos_y = idx_ref[1:2, cols] + tap
-                pos_z = idx_ref[2:3, cols] + tap
-                wy = w_ref[1, :, cols]
-                wz = w_ref[2, :, cols]
-                row_8 = lax.broadcasted_iota(jnp.int32, (8, SUB), 0)
-                line_z = jnp.zeros((8, SUB), F32)
-                ghost_y = jnp.zeros((8, SUB), F32)
-                row_y = lax.broadcasted_iota(jnp.int32, (len_y, SUB), 0)
-                line_y = jnp.zeros((len_y, SUB), F32)
-                for t in range(4):
-                    line_z = jnp.where(row_8 == pos_z[t:t + 1], wz[t:t + 1], line_z)
-                    ghost_y = jnp.where(row_8 + len_y == pos_y[t:t + 1], wy[t:t + 1], ghost_y)
-                    line_y = jnp.where(row_y == pos_y[t:t + 1], wy[t:t + 1], line_y)
-                line_ref[pl.ds(0, len_y), cols] = line_y
-                line_ref[pl.ds(len_y, 8), cols] = ghost_y
-                line_ref[pl.ds(len_y + 8, 8), cols] = line_z
-            else:
-                line_y = line_ref[pl.ds(0, len_y), cols]
-                ghost_y = line_ref[pl.ds(len_y, 8), cols]
-                line_z = line_ref[pl.ds(len_y + 8, 8), cols]
-            for k, z in enumerate(planes):
-                high, low = split_bf16(line_y * line_z[z:z + 1])
-                ph_ref[slot, k * len_y:(k + 1) * len_y, :] = high
-                pl_ref[slot, k * len_y:(k + 1) * len_y, :] = low
+                ahead = row_16 - idx_ref[0:1, cols]
+                taps = w_ref[0, :, cols] * weight
+                high, low = split_bf16(pick(ahead, taps))
+                tile_x = (-(ahead >> 4) & 15).astype(F32).astype(BF16)
+                for r in range(grid_n // 16):
+                    hit = tile_x == r
+                    near_ref[slot, 0, 16 * r:16 * r + 16, :] = jnp.where(hit, high, zero_16)
+                    near_ref[slot, 1, 16 * r:16 * r + 16, :] = jnp.where(hit, low, zero_16)
+                xh_ref[cols, :] = near_ref[slot, 0].T
+                xl_ref[cols, :] = near_ref[slot, 1].T
+            ahead = row_16 - idx_ref[1:2, cols]
+            line_y = pick(ahead, w_ref[1, :, cols])
+            tile = -(ahead >> 4)
+            ghost_y = jnp.where(tile[:8] == len_y // 16, line_y[:8], 0.0)
+            tile_y = tile.astype(F32).astype(BF16)
+            line_z = pick(row_16[:8] - idx_ref[2:3, cols], w_ref[2, :, cols], False)
+            sides = [split_bf16(line_y * line_z[z:z + 1]) for z in planes]
+            for r in range(len_y // 16):
+                hit = tile_y == r
+                for k, side in enumerate(sides):
+                    first = k * len_y + 16 * r
+                    ph_ref[slot, first:first + 16, :] = jnp.where(hit, side[0], zero_16)
+                    pl_ref[slot, first:first + 16, :] = jnp.where(hit, side[1], zero_16)
             ghosts = [ghost_y * line_z[z:z + 1] for z in planes]
             if len(planes) % 2:
                 ghosts.append(jnp.zeros((8, SUB), F32))
@@ -162,7 +159,10 @@
             rows = pl.ds(0, top + ghost_rows(group))
             ph_ref[slot, top:top + ghost_rows(group), :] = high
             pl_ref[slot, top:top + ghost_rows(group), :] = low
-            part = dot3((ph_ref[slot, rows, :], pl_ref[slot, rows, :]), (xh_ref[cols, :], xl_ref[cols, :]))
+            if group == 0:
+                part = dot3((ph_ref[slot, rows, :], pl_ref[slot, rows, :]), (near_ref[slot, 0], near_ref[slot, 1]), 1)
+            else:
+                part = dot3((ph_ref[slot, rows, :], pl_ref[slot, rows, :]), (xh_ref[cols, :], xl_ref[cols, :]))
             total = part if total is None else total + part
         acc_refs[group][...] += total
 
@@ -332,8 +332,7 @@
             out_shape=[jax.ShapeDtypeStruct(influence.shape, F32), jax.ShapeDtypeStruct((1,), F32)],
             scratch_shapes=[
                 pltpu.VMEM((1, slots), F32), pltpu.VMEM((1, slots), jnp.int32), pltpu.VMEM((3, slots), jnp.int32), pltpu.VMEM((3, 4, slots), F32),
-                pltpu.VMEM((grid_n // y_devs + 16, slots), F32),
-                pltpu.VMEM((slots, grid_n), BF16), pltpu.VMEM((slots, grid_n), BF16),
+                pltpu.VMEM((2, 2, grid_n, SUB), BF16), pltpu.VMEM((slots, grid_n), BF16), pltpu.VMEM((slots, grid_n), BF16),
                 pltpu.VMEM((2, rows[0], SUB), BF16), pltpu.VMEM((2, rows[0], SUB), BF16),
                 [pltpu.VMEM((r, grid_n), F32) for r in rows], [pltpu.VMEM((r, grid_n), F32) for r in rows],
                 pltpu.VMEM((2 * grid_n, grid_n), F32), pltpu.VMEM((2 * grid_n, grid_n), F32), pltpu.VMEM((2 * grid_n, 4 * half), F32),

time: 76.2 us -> 67.7 us (0.89)
  Pallas kernels: 71.8 us -> 63.3 us
    pallas_call x1, Pallas kernels: 71.8 us -> 63.3 us  [local_energy(): pl.pallas_call(functools.partial(energy_kernel, y_devs, z_devs), in_specs...]
where the time goes in v4:
time: 67.7 us; the launch traced here: 67.5 us
  Pallas kernels  63.3 us (94%)
  between operations  2.34 us (3%)
  local copies, waits for them, and re-layouts  1.87 us (3%)
    pallas_call x1, Pallas kernels, local_energy(): pl.pallas_call(functools.partial(energy_kernel, y_devs, z_devs), in_specs...  63.3 us
    unnamed x1, local copies, waits for them, and re-layouts  1.87 us

profile of v4, /device:TPU:1, one launch (start us, length us, event | category | flops | bytes accessed | tf_op | source)
XLA Modules:
  0.0 67.5 jit_solution(7216530347551750841)
XLA Ops:
  0.6 63.3 %energy.1 = (f32[128,4,256]{2,1,0:T(4,128)}, f32[1]{0:T(128)}) custom-call(f32[1,16384]{1,0:T(1,128)} %bitcast.6, s32[1,16384]{1,0:T(1,128)} %bitcast.7, s32[3,16384]{1,0:T(4,128)} %bitcast.5, f32[3,4,16384]{2,1,0:T(4,128)} %bitcast.4, f32[128,4,256]{2,1,0:T(4,128)} %bc_hbm.1, bf16[2,2,256,256]{3,2,1,0:T(8,128)(2,1)} %constant.6.clone.tx_hbm, ...), custom_call_target="tpu_custom_call" | custom-call | tf_op jit(solution)/shard_map/energy/pallas_call | solution.py:328
  63.9 1.9 %copy.12 = f32[128,4,256]{2,1,0:T(4,128)} copy(f32[128,4,256]{2,1,0:T(4,128)} %get-tuple-element.4) | data formatting | bytes 1048576

commit v5 on v4

--- a/solution.py
+++ b/solution.py
@@ -88,6 +88,10 @@
     def chip(step):
         return (my_z + step) & (z_devs - 1)
 
+    def far_first(start):
+        pl.loop(z_devs // 2, z_devs)(start)
+        pl.loop(1, z_devs // 2)(start)
+
     def slot_loads(piece):
         cols = pl.ds(0, EARLY) if piece == 0 else pl.ds(EARLY, slots - EARLY)
         return [pltpu.make_async_copy(hbm.at[lead + (cols,)], ref.at[lead + (cols,)], early_sem.at[piece, k])
@@ -99,7 +103,8 @@
 
     @pl.loop(1, z_devs)
     def _(step):
-        pl.semaphore_signal(barrier, inc=1, device_id={'zdom': chip(step)}, device_id_type=MESH)
+        for core in range(y_devs):
+            pl.semaphore_signal(barrier, inc=1, device_id={'zdom': chip(step), 'ydom': core}, device_id_type=MESH)
 
     pl.semaphore_signal(barrier, inc=1, device_id=partner, device_id_type=MESH)
 
@@ -195,11 +200,12 @@
         last = group // 2
         scale_ref[last, pl.ds(group % 2, 1)] = jnp.broadcast_to(peak * (1.0 / CODE_MAX), (1, 128))
 
-        @pl.loop(1, z_devs)
-        def _(step):
+        def start(step):
             send(group, step).start()
             if group:
                 send_scale(last, step).start()
+
+        far_first(start)
 
         recv_refs[group][my_z] = code_refs[group][my_z]
         if group:
@@ -253,7 +259,7 @@
                     transform_send(group - 1)
 
         if group == 0:
-            pl.semaphore_wait(barrier, z_devs)
+            pl.semaphore_wait(barrier, y_devs * z_devs - 1)
             for load in loads:
                 load.wait()
         swap(group).start()
@@ -273,36 +279,36 @@
     fold(1, jnp.concatenate([late, jnp.zeros_like(late)], axis=1))
     transform_z(1)
 
-    row = jnp.zeros((8, grid_n), F32)
+    row = jnp.zeros((8, half), F32)
     for ky in range(4):
         cols = pl.ds(ky * half, half)
         real, imag = zed_ref[pl.ds(0, grid_n), cols], zed_ref[pl.ds(grid_n, grid_n), cols]
-        value = 0.5 * bc_ref[:, ky, :] * (real * real + imag * imag).T
-        ek_ref[:, ky, :] = value
-        row += jnp.sum(value.reshape(half // 8, 8, grid_n), axis=0)
+        power = real * real + imag * imag
+        for part in range(2):
+            place = pl.ds(4 * part + ky, half, stride=8)
+            value = bc_ref[place, :] * power[part * half:(part + 1) * half].T
+            ek_ref[place, :] = value
+            row += jnp.sum(value.reshape(half // 8, 8, half), axis=0)
     store = pltpu.make_async_copy(ek_ref, ek_hbm, load_sem.at[0])
     store.start()
-    row_ref[0] = jnp.broadcast_to(jnp.sum(row[:, :half] + row[:, half:], axis=0, keepdims=True), (8, half))
-
-    def pair_copy():
-        return pltpu.make_async_remote_copy(src_ref=row_ref.at[0], dst_ref=row_ref.at[1], send_sem=row_sem.at[0], recv_sem=row_sem.at[1], device_id=partner, device_id_type=MESH)
-
-    def row_copy(step):
-        return pltpu.make_async_remote_copy(src_ref=row_ref.at[2, pl.ds(0, 1)], dst_ref=rrow_ref.at[my_z, pl.ds(0, 1)], send_sem=row_sem.at[2], recv_sem=row_sem.at[3], device_id={'zdom': chip(step)}, device_id_type=MESH)
-
-    pair_copy().start()
-    pair_copy().wait()
-    row_ref[2] = row_ref[0] + row_ref[1]
-
-    @pl.loop(1, z_devs)
-    def _(step):
-        row_copy(step).start()
-
-    rrow_ref[my_z, pl.ds(0, 1)] = row_ref[2, pl.ds(0, 1)]
-    others = rrow_ref.at[pl.ds(0, z_devs - 1), pl.ds(0, 1)]
-    pltpu.make_async_copy(others, others, row_sem.at[3]).wait()
-    sum_ref[0] = jnp.sum(rrow_ref[:, pl.ds(0, 1), :]) * (1.0 / (grid_n * grid_n * grid_n))
-    await_all(others, row_sem.at[2])
+    row_ref[...] = jnp.broadcast_to(jnp.sum(row, axis=0, keepdims=True), (8, half))
+
+    me = my_z * y_devs + my_y
+    others = rrow_ref.at[pl.ds(0, y_devs * z_devs - 1), pl.ds(0, 1)]
+
+    def row_copy(device):
+        return pltpu.make_async_remote_copy(src_ref=row_ref.at[pl.ds(0, 1)], dst_ref=rrow_ref.at[me, pl.ds(0, 1)], send_sem=row_sem.at[0], recv_sem=row_sem.at[1], device_id=device, device_id_type=MESH)
+
+    def start(step):
+        for core in range(y_devs):
+            row_copy({'zdom': chip(step), 'ydom': core}).start()
+
+    far_first(start)
+    row_copy(partner).start()
+    rrow_ref[me, pl.ds(0, 1)] = row_ref[pl.ds(0, 1)]
+    await_all(others, row_sem.at[1])
+    sum_ref[0] = jnp.sum(rrow_ref[:, pl.ds(0, 1), :]) * (0.5 / (grid_n * grid_n * grid_n))
+    await_all(others, row_sem.at[0])
     for group in range(n_groups):
         await_all(code_refs[group].at[pl.ds(0, z_devs - 1)], send_sem.at[group])
     for last in range(2):
@@ -325,11 +331,12 @@
         any_spec = pl.BlockSpec(memory_space=pl.ANY)
         rows = [len(GROUPS[g]) * (grid_n // y_devs) + ghost_rows(g) for g in range(n_groups)]
         codes = [pltpu.VMEM((z_devs, len(planes), 8, half), jnp.int16) for planes in GROUPS]
+        tiles = jnp.swapaxes(influence.reshape(half, 4, 2, half), 1, 2).reshape(8 * half, half)
         mode_energy, energy = pl.pallas_call(
             functools.partial(energy_kernel, y_devs, z_devs),
             in_specs=[any_spec] * 8,
             out_specs=[any_spec, pl.BlockSpec(memory_space=pltpu.SMEM)],
-            out_shape=[jax.ShapeDtypeStruct(influence.shape, F32), jax.ShapeDtypeStruct((1,), F32)],
+            out_shape=[jax.ShapeDtypeStruct((8 * half, half), F32), jax.ShapeDtypeStruct((1,), F32)],
             scratch_shapes=[
                 pltpu.VMEM((1, slots), F32), pltpu.VMEM((1, slots), jnp.int32), pltpu.VMEM((3, slots), jnp.int32), pltpu.VMEM((3, 4, slots), F32),
                 pltpu.VMEM((2, 2, grid_n, SUB), BF16), pltpu.VMEM((slots, grid_n), BF16), pltpu.VMEM((slots, grid_n), BF16),
@@ -339,17 +346,18 @@
                 codes, codes,
                 pltpu.VMEM((2, 2, 128), F32), pltpu.VMEM((2, z_devs, 2, 128), F32),
                 pltpu.VMEM((2, z_devs * 16, half), F32), pltpu.VMEM((2 * grid_n, 4 * half), F32),
-                pltpu.VMEM(influence.shape, F32), pltpu.VMEM(influence.shape, F32),
+                pltpu.VMEM((8 * half, half), F32), pltpu.VMEM((8 * half, half), F32),
                 pltpu.VMEM(table_x.shape[1:], BF16), pltpu.VMEM(table_y.shape, BF16), pltpu.VMEM(table_z.shape, BF16),
-                pltpu.VMEM((3, 8, 128), F32), pltpu.VMEM((z_devs, 8, 128), F32),
+                pltpu.VMEM((8, 128), F32), pltpu.VMEM((y_devs * z_devs, 8, 128), F32),
                 pltpu.SemaphoreType.DMA((2, 4)), pltpu.SemaphoreType.DMA((4,)), pltpu.SemaphoreType.DMA((2, n_groups)),
                 pltpu.SemaphoreType.DMA((n_groups,)), pltpu.SemaphoreType.DMA((n_groups,)),
                 pltpu.SemaphoreType.DMA((2,)), pltpu.SemaphoreType.DMA((2,)),
-                pltpu.SemaphoreType.DMA((4,)),
+                pltpu.SemaphoreType.DMA((2,)),
             ],
             compiler_params=pltpu.CompilerParams(collective_id=0, has_side_effects=True, vmem_limit_bytes=60 * 1024 * 1024),
             name="energy",
-        )(charge.reshape(1, slots), real_mask.reshape(1, slots), grid_idx.T, jnp.transpose(spline_w, (1, 2, 0)), influence, jnp.asarray(table_x), jnp.asarray(table_y), jnp.asarray(table_z))
-        return mode_energy, energy
+        )(charge.reshape(1, slots), real_mask.reshape(1, slots), grid_idx.T, jnp.transpose(spline_w, (1, 2, 0)), tiles, jnp.asarray(table_x), jnp.asarray(table_y), jnp.asarray(table_z))
+        mode_energy = lax.optimization_barrier(0.5 * mode_energy)
+        return jnp.swapaxes(mode_energy.reshape(half, 2, 4, half), 1, 2).reshape(influence.shape), energy
 
     return jax.shard_map(local_energy, mesh=mesh, in_specs=(slot_spec, slot_spec, P(('sys', 'ydom', 'zdom'), None), P(('sys', 'ydom', 'zdom'), None, None), mode_spec), out_specs=(mode_spec, P('sys')), check_vma=False)

time: 67.7 us -> 66.8 us (0.987)
  other arithmetic: 0 us -> 1.87 us
  local copies, waits for them, and re-layouts: 1.87 us -> 0 us
  Pallas kernels: 63.3 us -> 62.4 us
    mul x0 -> x1, other arithmetic: none -> 1.87 us  [local_energy(): mode_energy = lax.optimization_barrier(0.5 * mode_energy)]
    unnamed x1 -> x0, local copies, waits for them, and re-layouts: 1.87 us -> none
    pallas_call x1, Pallas kernels: 63.3 us -> 62.4 us  [local_energy(): pl.pallas_call(functools.partial(energy_kernel, y_devs, z_devs), in_specs...]
where the time goes in v5:
time: 66.8 us; the launch traced here: 66.6 us
  Pallas kernels  62.4 us (93%)
  between operations  2.34 us (4%)
  other arithmetic  1.87 us (3%)
    pallas_call x1, Pallas kernels, local_energy(): pl.pallas_call(functools.partial(energy_kernel, y_devs, z_devs), in_specs...  62.4 us
    mul x1, other arithmetic, local_energy(): mode_energy = lax.optimization_barrier(0.5 * mode_energy)  1.87 us

profile of v5, /device:TPU:1, one launch (start us, length us, event | category | flops | bytes accessed | tf_op | source)
XLA Modules:
  0.0 66.6 jit_solution(15946919528649094142)
XLA Ops:
  0.6 62.4 %energy.1 = (f32[1024,128]{1,0:T(8,128)}, f32[1]{0:T(128)}) custom-call(f32[1,16384]{1,0:T(1,128)} %bitcast.18, s32[1,16384]{1,0:T(1,128)} %bitcast.19, s32[3,16384]{1,0:T(4,128)} %bitcast.17, f32[3,4,16384]{2,1,0:T(4,128)} %bitcast.14, f32[1024,128]{1,0:T(8,128)} %bitcast.15, bf16[2,2,256,256]{3,2,1,0:T(8,128)(2,1)} %constant.8.clone.tx_hbm, ...), custom_call_target="tpu_custom_call" | custom-call | tf_op jit(solution)/shard_map/energy/pallas_call | solution.py:335
  63.0 1.9 %broadcast_multiply_fusion = f32[1024,128]{1,0:T(8,128)} fusion(f32[1024,128]{1,0:T(8,128)} %get-tuple-element.4), kind=kLoop, calls=%fused_computation | loop fusion | flops 131072 | bytes 1048576 | tf_op jit(solution)/shard_map/mul | solution.py:360

commit v6 on v5

--- a/solution.py
+++ b/solution.py
@@ -11,9 +11,9 @@
 F32 = jnp.float32
 BF16 = jnp.bfloat16
 SUB = 256
-CHUNK = 1024
+CHUNK = 2048
 GROUPS = ((0, 1, 2, 3), (4, 5), (6,))
-STEP_AT = (0, 5, 7)
+STEP_AT = (0, 2, 3)
 EARLY = 2048
 CODE_MAX = 32767.0
 MESH = pl.DeviceIdType.MESH
@@ -70,10 +70,10 @@
     return -(-8 * len(GROUPS[group]) // 16) * 16
 
 
-def energy_kernel(y_devs, z_devs, q_hbm, m_hbm, idx_hbm, w_hbm, bc_hbm, tx_hbm, ty_hbm, tz_hbm, ek_hbm, sum_ref,
+def energy_kernel(y_devs, z_devs, q_hbm, m_hbm, idx_hbm, w_hbm, bc_hbm, tx_hbm, ty_hbm, tz_hbm, ek_ref, sum_ref,
                   q_ref, m_ref, idx_ref, w_ref, near_ref, xh_ref, xl_ref, ph_ref, pl_ref, acc_refs, got_refs, grid_ref, mid_ref, mode_ref,
                   code_refs, recv_refs, scale_ref, rscale_ref,
-                  deq_ref, zed_ref, bc_ref, ek_ref, tx_ref, ty_ref, tz_ref, row_ref, rrow_ref,
+                  deq_ref, zed_ref, bc_ref, tx_ref, ty_ref, tz_ref, row_ref, rrow_ref,
                   early_sem, load_sem, swap_sem, send_sem, recv_sem, ssend_sem, srecv_sem, row_sem):
     my_y = lax.axis_index('ydom')
     my_z = lax.axis_index('zdom')
@@ -103,8 +103,7 @@
 
     @pl.loop(1, z_devs)
     def _(step):
-        for core in range(y_devs):
-            pl.semaphore_signal(barrier, inc=1, device_id={'zdom': chip(step), 'ydom': core}, device_id_type=MESH)
+        pl.semaphore_signal(barrier, inc=1, device_id={'zdom': chip(step)}, device_id_type=MESH)
 
     pl.semaphore_signal(barrier, inc=1, device_id=partner, device_id_type=MESH)
 
@@ -259,7 +258,7 @@
                     transform_send(group - 1)
 
         if group == 0:
-            pl.semaphore_wait(barrier, y_devs * z_devs - 1)
+            pl.semaphore_wait(barrier, z_devs)
             for load in loads:
                 load.wait()
         swap(group).start()
@@ -289,23 +288,19 @@
             value = bc_ref[place, :] * power[part * half:(part + 1) * half].T
             ek_ref[place, :] = value
             row += jnp.sum(value.reshape(half // 8, 8, half), axis=0)
-    store = pltpu.make_async_copy(ek_ref, ek_hbm, load_sem.at[0])
-    store.start()
-    row_ref[...] = jnp.broadcast_to(jnp.sum(row, axis=0, keepdims=True), (8, half))
-
-    me = my_z * y_devs + my_y
-    others = rrow_ref.at[pl.ds(0, y_devs * z_devs - 1), pl.ds(0, 1)]
-
-    def row_copy(device):
-        return pltpu.make_async_remote_copy(src_ref=row_ref.at[pl.ds(0, 1)], dst_ref=rrow_ref.at[me, pl.ds(0, 1)], send_sem=row_sem.at[0], recv_sem=row_sem.at[1], device_id=device, device_id_type=MESH)
+    row_ref[0] = jnp.broadcast_to(jnp.sum(row, axis=0, keepdims=True), (8, half))
+
+    others = rrow_ref.at[pl.ds(0, z_devs - 1), pl.ds(0, 1)]
+    pair = pltpu.make_async_remote_copy(src_ref=row_ref.at[0, pl.ds(0, 1)], dst_ref=row_ref.at[1, pl.ds(0, 1)], send_sem=row_sem.at[2], recv_sem=row_sem.at[3], device_id=partner, device_id_type=MESH)
+    pair.start()
+    pair.wait()
+    row_ref[2] = row_ref[0] + row_ref[1]
 
     def start(step):
-        for core in range(y_devs):
-            row_copy({'zdom': chip(step), 'ydom': core}).start()
+        pltpu.make_async_remote_copy(src_ref=row_ref.at[2, pl.ds(0, 1)], dst_ref=rrow_ref.at[my_z, pl.ds(0, 1)], send_sem=row_sem.at[0], recv_sem=row_sem.at[1], device_id={'zdom': chip(step)}, device_id_type=MESH).start()
 
     far_first(start)
-    row_copy(partner).start()
-    rrow_ref[me, pl.ds(0, 1)] = row_ref[pl.ds(0, 1)]
+    rrow_ref[my_z, pl.ds(0, 1)] = row_ref[2, pl.ds(0, 1)]
     await_all(others, row_sem.at[1])
     sum_ref[0] = jnp.sum(rrow_ref[:, pl.ds(0, 1), :]) * (0.5 / (grid_n * grid_n * grid_n))
     await_all(others, row_sem.at[0])
@@ -313,7 +308,6 @@
         await_all(code_refs[group].at[pl.ds(0, z_devs - 1)], send_sem.at[group])
     for last in range(2):
         await_all(rscale_ref.at[last, pl.ds(0, z_devs - 1), pl.ds(0, 2 - last)], ssend_sem.at[last])
-    store.wait()
 
 
 def solution(mesh):
@@ -335,8 +329,8 @@
         mode_energy, energy = pl.pallas_call(
             functools.partial(energy_kernel, y_devs, z_devs),
             in_specs=[any_spec] * 8,
-            out_specs=[any_spec, pl.BlockSpec(memory_space=pltpu.SMEM)],
-            out_shape=[jax.ShapeDtypeStruct((8 * half, half), F32), jax.ShapeDtypeStruct((1,), F32)],
+            out_specs=[pl.BlockSpec(memory_space=pltpu.VMEM), pl.BlockSpec(memory_space=pltpu.SMEM)],
+            out_shape=[pltpu.VMEM((8 * half, half), F32), jax.ShapeDtypeStruct((1,), F32)],
             scratch_shapes=[
                 pltpu.VMEM((1, slots), F32), pltpu.VMEM((1, slots), jnp.int32), pltpu.VMEM((3, slots), jnp.int32), pltpu.VMEM((3, 4, slots), F32),
                 pltpu.VMEM((2, 2, grid_n, SUB), BF16), pltpu.VMEM((slots, grid_n), BF16), pltpu.VMEM((slots, grid_n), BF16),
@@ -346,13 +340,13 @@
                 codes, codes,
                 pltpu.VMEM((2, 2, 128), F32), pltpu.VMEM((2, z_devs, 2, 128), F32),
                 pltpu.VMEM((2, z_devs * 16, half), F32), pltpu.VMEM((2 * grid_n, 4 * half), F32),
-                pltpu.VMEM((8 * half, half), F32), pltpu.VMEM((8 * half, half), F32),
+                pltpu.VMEM((8 * half, half), F32),
                 pltpu.VMEM(table_x.shape[1:], BF16), pltpu.VMEM(table_y.shape, BF16), pltpu.VMEM(table_z.shape, BF16),
-                pltpu.VMEM((8, 128), F32), pltpu.VMEM((y_devs * z_devs, 8, 128), F32),
+                pltpu.VMEM((3, 8, 128), F32), pltpu.VMEM((z_devs, 8, 128), F32),
                 pltpu.SemaphoreType.DMA((2, 4)), pltpu.SemaphoreType.DMA((4,)), pltpu.SemaphoreType.DMA((2, n_groups)),
                 pltpu.SemaphoreType.DMA((n_groups,)), pltpu.SemaphoreType.DMA((n_groups,)),
                 pltpu.SemaphoreType.DMA((2,)), pltpu.SemaphoreType.DMA((2,)),
-                pltpu.SemaphoreType.DMA((2,)),
+                pltpu.SemaphoreType.DMA((4,)),
             ],
             compiler_params=pltpu.CompilerParams(collective_id=0, has_side_effects=True, vmem_limit_bytes=60 * 1024 * 1024),
             name="energy",

time: 66.8 us -> 61.4 us (0.919)
  Pallas kernels: 62.4 us -> 58.1 us
  other arithmetic: 1.87 us -> 0.83 us
    pallas_call x1, Pallas kernels: 62.4 us -> 58.1 us  [local_energy(): pl.pallas_call(functools.partial(energy_kernel, y_devs, z_devs), in_specs...]
    mul x1, other arithmetic: 1.87 us -> 0.83 us  [local_energy(): mode_energy = lax.optimization_barrier(0.5 * mode_energy)]
where the time goes in v6:
time: 61.4 us; the launch traced here: 61.2 us
  Pallas kernels  58.1 us (95%)
  between operations  2.33 us (4%)
  other arithmetic  0.83 us (1%)
    pallas_call x1, Pallas kernels, local_energy(): pl.pallas_call(functools.partial(energy_kernel, y_devs, z_devs), in_specs...  58.1 us

profile of v6, /device:TPU:1, one launch (start us, length us, event | category | flops | bytes accessed | tf_op | source)
XLA Modules:
  0.0 61.2 jit_solution(2742637327466637920)
XLA Ops:
  0.6 58.1 %energy.1 = (f32[1024,128]{1,0:T(8,128)S(1)}, f32[1]{0:T(128)}) custom-call(f32[1,16384]{1,0:T(1,128)} %bitcast.18, s32[1,16384]{1,0:T(1,128)} %bitcast.19, s32[3,16384]{1,0:T(4,128)} %bitcast.17, f32[3,4,16384]{2,1,0:T(4,128)} %bitcast.14, f32[1024,128]{1,0:T(8,128)} %bitcast.15, bf16[2,2,256,256]{3,2,1,0:T(8,128)(2,1)} %constant.8.clone.tx_hbm, ...), custom_call_target="tpu_custom_call" | custom-call | tf_op jit(solution)/shard_map/energy/pallas_call | solution.py:329
  58.7 0.8 %broadcast_multiply_fusion = f32[1024,128]{1,0:T(8,128)} fusion(f32[1024,128]{1,0:T(8,128)S(1)} %get-tuple-element.4), kind=kLoop, calls=%fused_computation | loop fusion | flops 131072 | bytes 1048576 | tf_op jit(solution)/shard_map/mul | solution.py:354

commit v7 on v6

--- a/solution.py
+++ b/solution.py
@@ -72,9 +72,9 @@
 
 def energy_kernel(y_devs, z_devs, q_hbm, m_hbm, idx_hbm, w_hbm, bc_hbm, tx_hbm, ty_hbm, tz_hbm, ek_ref, sum_ref,
                   q_ref, m_ref, idx_ref, w_ref, near_ref, xh_ref, xl_ref, ph_ref, pl_ref, acc_refs, got_refs, grid_ref, mid_ref, mode_ref,
-                  code_refs, recv_refs, scale_ref, rscale_ref,
+                  code_refs, recv_refs,
                   deq_ref, zed_ref, bc_ref, tx_ref, ty_ref, tz_ref, row_ref, rrow_ref,
-                  early_sem, load_sem, swap_sem, send_sem, recv_sem, ssend_sem, srecv_sem, row_sem):
+                  early_sem, load_sem, swap_sem, send_sem, recv_sem, row_sem):
     my_y = lax.axis_index('ydom')
     my_z = lax.axis_index('zdom')
     grid_n = xh_ref.shape[1]
@@ -115,12 +115,12 @@
     def swap(group):
         return pltpu.make_async_remote_copy(src_ref=acc_refs[group], dst_ref=got_refs[group], send_sem=swap_sem.at[0, group], recv_sem=swap_sem.at[1, group], device_id=partner, device_id_type=MESH)
 
+    def used(group):
+        return pl.ds(0, 8 * len(GROUPS[group]) + 2)
+
     def send(group, step):
         other = chip(step)
-        return pltpu.make_async_remote_copy(src_ref=code_refs[group].at[other], dst_ref=recv_refs[group].at[my_z], send_sem=send_sem.at[group], recv_sem=recv_sem.at[group], device_id={'zdom': other}, device_id_type=MESH)
-
-    def send_scale(last, step):
-        return pltpu.make_async_remote_copy(src_ref=scale_ref.at[last, pl.ds(0, 2 - last)], dst_ref=rscale_ref.at[last, my_z, pl.ds(0, 2 - last)], send_sem=ssend_sem.at[last], recv_sem=srecv_sem.at[last], device_id={'zdom': chip(step)}, device_id_type=MESH)
+        return pltpu.make_async_remote_copy(src_ref=code_refs[group].at[other, used(group)], dst_ref=recv_refs[group].at[my_z, used(group)], send_sem=send_sem.at[group], recv_sem=recv_sem.at[group], device_id={'zdom': other}, device_id_type=MESH)
 
     def spread(group, base):
         planes = GROUPS[group]
@@ -192,36 +192,31 @@
             modes = dot3((ty_ref[0], ty_ref[1]), split_bf16(jnp.concatenate(columns, axis=1)))
             mode_ref[:, pl.ds(first * half, count * half)] = modes
             peak = jnp.maximum(peak, jnp.max(jnp.abs(modes), keepdims=True))
-        gain = CODE_MAX / peak
-        for k in range(len(planes)):
-            codes = jnp.round(mode_ref[:, pl.ds(k * half, half)] * gain).astype(jnp.int32).astype(jnp.int16)
-            code_refs[group][:, k] = codes.reshape(z_devs, 8, half)
-        last = group // 2
-        scale_ref[last, pl.ds(group % 2, 1)] = jnp.broadcast_to(peak * (1.0 / CODE_MAX), (1, 128))
+        power = jnp.ceil(jnp.log2(peak * (1.0 / CODE_MAX)) + 1e-3)
+        gain = jnp.exp2(-power)
+        for first in range(0, len(planes), 2):
+            count = min(2, len(planes) - first)
+            scaled = [(mode_ref[:, pl.ds((first + k) * half, half)] * gain).reshape(z_devs, 8, half) for k in range(count)]
+            codes = jnp.round(jnp.concatenate(scaled, axis=1)).astype(jnp.int32).astype(jnp.int16)
+            code_refs[group][:, pl.ds(8 * first, 8 * count), :] = codes
+        code_refs[group][:, pl.ds(8 * len(planes), 2), :] = jnp.broadcast_to(power.astype(jnp.int32), (z_devs, 2, half)).astype(jnp.int16)
 
         def start(step):
             send(group, step).start()
-            if group:
-                send_scale(last, step).start()
 
         far_first(start)
-
         recv_refs[group][my_z] = code_refs[group][my_z]
-        if group:
-            rscale_ref[last, my_z] = scale_ref[last]
 
     def await_all(ref, sem):
         pltpu.make_async_copy(ref, ref, sem).wait()
 
     def await_codes(group):
-        await_all(recv_refs[group].at[pl.ds(0, z_devs - 1)], recv_sem.at[group])
-
-    def await_scale(last):
-        await_all(rscale_ref.at[last, pl.ds(0, z_devs - 1), pl.ds(0, 2 - last)], srecv_sem.at[last])
-
-    def decode(group, planes):
-        codes = recv_refs[group][:, planes].astype(jnp.int32).astype(F32)
-        return codes * rscale_ref[group // 2, :, pl.ds(group % 2, 1), :].reshape(z_devs, 1, 1, half)
+        await_all(recv_refs[group].at[pl.ds(0, z_devs - 1), used(group)], recv_sem.at[group])
+
+    def decode(group, first, count):
+        powers = recv_refs[group][:, pl.ds(8 * len(GROUPS[group]), 2), :].astype(jnp.int32).astype(F32)
+        codes = recv_refs[group][:, pl.ds(8 * first, 8 * count), :].astype(jnp.int32).astype(F32)
+        return codes * jnp.exp2(powers[:, :1, :])
 
     def fold(part, planes):
         rows = z_devs * 16
@@ -266,15 +261,13 @@
 
     rows = z_devs * 16
     await_codes(0)
-    await_scale(0)
     for part in range(2):
-        deq_ref[part] = decode(0, slice(2 * part, 2 * part + 2)).reshape(rows, half)
+        deq_ref[part] = decode(0, 2 * part, 2).reshape(rows, half)
     await_codes(1)
-    fold(0, decode(1, slice(0, 2)))
+    fold(0, decode(1, 0, 2))
     transform_z(0)
     await_codes(2)
-    await_scale(1)
-    late = decode(2, slice(0, 1))
+    late = decode(2, 0, 1)
     fold(1, jnp.concatenate([late, jnp.zeros_like(late)], axis=1))
     transform_z(1)
 
@@ -305,9 +298,7 @@
     sum_ref[0] = jnp.sum(rrow_ref[:, pl.ds(0, 1), :]) * (0.5 / (grid_n * grid_n * grid_n))
     await_all(others, row_sem.at[0])
     for group in range(n_groups):
-        await_all(code_refs[group].at[pl.ds(0, z_devs - 1)], send_sem.at[group])
-    for last in range(2):
-        await_all(rscale_ref.at[last, pl.ds(0, z_devs - 1), pl.ds(0, 2 - last)], ssend_sem.at[last])
+        await_all(code_refs[group].at[pl.ds(0, z_devs - 1), used(group)], send_sem.at[group])
 
 
 def solution(mesh):
@@ -324,7 +315,7 @@
         table_x, table_y, table_z = dft_tables(grid_n, y_devs, z_devs)
         any_spec = pl.BlockSpec(memory_space=pl.ANY)
         rows = [len(GROUPS[g]) * (grid_n // y_devs) + ghost_rows(g) for g in range(n_groups)]
-        codes = [pltpu.VMEM((z_devs, len(planes), 8, half), jnp.int16) for planes in GROUPS]
+        codes = [pltpu.VMEM((z_devs, -(-(8 * len(planes) + 2) // 16) * 16, half), jnp.int16) for planes in GROUPS]
         tiles = jnp.swapaxes(influence.reshape(half, 4, 2, half), 1, 2).reshape(8 * half, half)
         mode_energy, energy = pl.pallas_call(
             functools.partial(energy_kernel, y_devs, z_devs),
@@ -338,14 +329,12 @@
                 [pltpu.VMEM((r, grid_n), F32) for r in rows], [pltpu.VMEM((r, grid_n), F32) for r in rows],
                 pltpu.VMEM((2 * grid_n, grid_n), F32), pltpu.VMEM((2 * grid_n, grid_n), F32), pltpu.VMEM((2 * grid_n, 4 * half), F32),
                 codes, codes,
-                pltpu.VMEM((2, 2, 128), F32), pltpu.VMEM((2, z_devs, 2, 128), F32),
                 pltpu.VMEM((2, z_devs * 16, half), F32), pltpu.VMEM((2 * grid_n, 4 * half), F32),
                 pltpu.VMEM((8 * half, half), F32),
                 pltpu.VMEM(table_x.shape[1:], BF16), pltpu.VMEM(table_y.shape, BF16), pltpu.VMEM(table_z.shape, BF16),
                 pltpu.VMEM((3, 8, 128), F32), pltpu.VMEM((z_devs, 8, 128), F32),
                 pltpu.SemaphoreType.DMA((2, 4)), pltpu.SemaphoreType.DMA((4,)), pltpu.SemaphoreType.DMA((2, n_groups)),
                 pltpu.SemaphoreType.DMA((n_groups,)), pltpu.SemaphoreType.DMA((n_groups,)),
-                pltpu.SemaphoreType.DMA((2,)), pltpu.SemaphoreType.DMA((2,)),
                 pltpu.SemaphoreType.DMA((4,)),
             ],
             compiler_params=pltpu.CompilerParams(collective_id=0, has_side_effects=True, vmem_limit_bytes=60 * 1024 * 1024),

time: 61.4 us -> 60.8 us (level)
  no operation moved by 1% of the time
where the time goes in v7:
time: 60.8 us; the launch traced here: 60.6 us
  Pallas kernels  57.5 us (95%)
  between operations  2.33 us (4%)
  other arithmetic  0.83 us (1%)
    pallas_call x1, Pallas kernels, local_energy(): pl.pallas_call(functools.partial(energy_kernel, y_devs, z_devs), in_specs...  57.5 us

profile of v7, /device:TPU:1, one launch (start us, length us, event | category | flops | bytes accessed | tf_op | source)
XLA Modules:
  0.0 60.6 jit_solution(14581921091151306657)
XLA Ops:
  0.6 57.5 %energy.1 = (f32[1024,128]{1,0:T(8,128)S(1)}, f32[1]{0:T(128)}) custom-call(f32[1,16384]{1,0:T(1,128)} %bitcast.18, s32[1,16384]{1,0:T(1,128)} %bitcast.19, s32[3,16384]{1,0:T(4,128)} %bitcast.17, f32[3,4,16384]{2,1,0:T(4,128)} %bitcast.14, f32[1024,128]{1,0:T(8,128)} %bitcast.15, bf16[2,2,256,256]{3,2,1,0:T(8,128)(2,1)} %constant.8.clone.tx_hbm, ...), custom_call_target="tpu_custom_call" | custom-call | tf_op jit(solution)/shard_map/energy/pallas_call | solution.py:320
  58.1 0.8 %broadcast_multiply_fusion = f32[1024,128]{1,0:T(8,128)} fusion(f32[1024,128]{1,0:T(8,128)S(1)} %get-tuple-element.4), kind=kLoop, calls=%fused_computation | loop fusion | flops 131072 | bytes 1048576 | tf_op jit(solution)/shard_map/mul | solution.py:343

commit v8 on v7

--- a/solution.py
+++ b/solution.py
@@ -10,7 +10,7 @@
 
 F32 = jnp.float32
 BF16 = jnp.bfloat16
-SUB = 256
+SUB = 512
 CHUNK = 2048
 GROUPS = ((0, 1, 2, 3), (4, 5), (6,))
 STEP_AT = (0, 2, 3)
@@ -51,29 +51,34 @@
     freq = np.arange(grid_n)
     phase_x = (np.outer(x, freq) % grid_n) * turn
     table_x = np.stack([np_split(np.concatenate([np.cos(phase_x[:, i * len_y:(i + 1) * len_y]), -np.sin(phase_x[:, i * len_y:(i + 1) * len_y])], axis=1)) for i in range(y_devs)])
-    phase_y = (np.outer(freq, x) % grid_n) * turn
-    real = np.concatenate([np.cos(phase_y), np.sin(phase_y)], axis=1)
-    imag = np.concatenate([-np.sin(phase_y), np.cos(phase_y)], axis=1)
-    rows = np.stack([real.reshape(z_devs, len_z, 2 * grid_n), imag.reshape(z_devs, len_z, 2 * grid_n)], axis=1)
-    table_y = np_split(rows.reshape(2 * grid_n, 2 * grid_n))
-    table_z = []
-    for first in (0, 2):
-        pos = np.arange(z_devs)[:, None] * len_z + first + np.arange(2)[None, :]
+    table_y = []
+    for parity in range(2):
+        ky = (np.arange(z_devs)[None, :] * len_z + 2 * np.arange(2)[:, None] + parity).reshape(-1)
+        phase_y = (np.outer(ky, np.arange(grid_n // 2)) % grid_n) * turn
+        real = np.concatenate([np.cos(phase_y), np.sin(phase_y)], axis=1)
+        imag = np.concatenate([-np.sin(phase_y), np.cos(phase_y)], axis=1)
+        table_y.append(np_split(np.concatenate([real, imag], axis=0)))
+
+    def z_table(first, count):
+        pos = np.arange(z_devs)[:, None] * len_z + first + np.arange(count)[None, :]
         phase_z = ((freq[:, None, None] * pos[None]) % grid_n) * turn
         real = np.stack([np.cos(phase_z), np.sin(phase_z)], axis=3).reshape(grid_n, -1)
         imag = np.stack([-np.sin(phase_z), np.cos(phase_z)], axis=3).reshape(grid_n, -1)
-        table_z.append(np_split(np.concatenate([real, imag], axis=0)))
-    return table_x, table_y, np.stack(table_z)
+        return np_split(np.concatenate([real, imag], axis=0))
+
+    high, low = z_table(6, 1)
+    late_z = np.concatenate([high, high, low], axis=1)
+    return table_x, np.stack(table_y), np.stack([z_table(0, 2), z_table(2, 2)]), late_z
 
 
 def ghost_rows(group):
     return -(-8 * len(GROUPS[group]) // 16) * 16
 
 
-def energy_kernel(y_devs, z_devs, q_hbm, m_hbm, idx_hbm, w_hbm, bc_hbm, tx_hbm, ty_hbm, tz_hbm, ek_ref, sum_ref,
+def energy_kernel(y_devs, z_devs, q_hbm, m_hbm, idx_hbm, w_hbm, bc_hbm, tx_hbm, ty_hbm, tz_hbm, tl_hbm, ek_ref, sum_ref,
                   q_ref, m_ref, idx_ref, w_ref, near_ref, xh_ref, xl_ref, ph_ref, pl_ref, acc_refs, got_refs, grid_ref, mid_ref, mode_ref,
                   code_refs, recv_refs,
-                  deq_ref, zed_ref, bc_ref, tx_ref, ty_ref, tz_ref, row_ref, rrow_ref,
+                  deq_ref, zed_ref, bc_ref, tx_ref, ty_ref, tz_ref, tl_ref, late_ref, row_ref, rrow_ref,
                   early_sem, load_sem, swap_sem, send_sem, recv_sem, row_sem):
     my_y = lax.axis_index('ydom')
     my_z = lax.axis_index('zdom')
@@ -108,7 +113,7 @@
     pl.semaphore_signal(barrier, inc=1, device_id=partner, device_id_type=MESH)
 
     loads = [pltpu.make_async_copy(tx_hbm.at[my_y], tx_ref, load_sem.at[0]), pltpu.make_async_copy(ty_hbm, ty_ref, load_sem.at[1]),
-             pltpu.make_async_copy(tz_hbm, tz_ref, load_sem.at[2]), pltpu.make_async_copy(bc_hbm, bc_ref, load_sem.at[3])]
+             pltpu.make_async_copy(tz_hbm, tz_ref, load_sem.at[2]), pltpu.make_async_copy(bc_hbm, bc_ref, load_sem.at[3]), pltpu.make_async_copy(tl_hbm, tl_ref, load_sem.at[4])]
     for load in loads:
         load.start()
 
@@ -174,29 +179,32 @@
         planes = GROUPS[group]
         acc_ref, got_ref = acc_refs[group], got_refs[group]
         swap(group).wait()
-        mine, theirs = my_y * len_y, (1 - my_y) * len_y
+        sign = (1 - 2 * my_y).astype(F32)
         peak = jnp.full((1, 1), 1e-30, F32)
         for first in range(0, len(planes), 2):
             count = min(2, len(planes) - first)
             for k in range(count):
                 block = pl.ds((first + k) * len_y, len_y)
-                grid_ref[pl.ds(pl.multiple_of(k * grid_n + mine, len_y), len_y), :] = acc_ref[block, :]
-                grid_ref[pl.ds(pl.multiple_of(k * grid_n + theirs, len_y), len_y), :] = got_ref[block, :]
-            for k in range(count):
                 ghost = pl.ds(len(planes) * len_y + 8 * (first + k), 8)
-                grid_ref[pl.ds(pl.multiple_of(k * grid_n + theirs, len_y), 8), :] += acc_ref[ghost, :]
-                grid_ref[pl.ds(pl.multiple_of(k * grid_n + mine, len_y), 8), :] += got_ref[ghost, :]
+                even, odd = 2 * k * len_y, (2 * k + 1) * len_y
+                grid_ref[pl.ds(even, len_y), :] = acc_ref[block, :] + got_ref[block, :]
+                grid_ref[pl.ds(odd, len_y), :] = sign * (acc_ref[block, :] - got_ref[block, :])
+                grid_ref[pl.ds(even, 8), :] += acc_ref[ghost, :] + got_ref[ghost, :]
+                grid_ref[pl.ds(odd, 8), :] -= sign * (acc_ref[ghost, :] - got_ref[ghost, :])
             size = count * grid_n
             mid_ref[pl.ds(0, size), :] = dot3(split_bf16(grid_ref[pl.ds(0, size), :]), (tx_ref[0], tx_ref[1]))
-            columns = [jnp.concatenate([mid_ref[pl.ds(k * grid_n, grid_n), pl.ds(c * half, half)] for c in range(2)], axis=0) for k in range(count)]
-            modes = dot3((ty_ref[0], ty_ref[1]), split_bf16(jnp.concatenate(columns, axis=1)))
-            mode_ref[:, pl.ds(first * half, count * half)] = modes
-            peak = jnp.maximum(peak, jnp.max(jnp.abs(modes), keepdims=True))
+            for parity in range(2):
+                columns = [jnp.concatenate([mid_ref[pl.ds((2 * k + parity) * len_y, len_y), pl.ds(c * half, half)] for c in range(2)], axis=0) for k in range(count)]
+                modes = dot3((ty_ref[parity, 0], ty_ref[parity, 1]), split_bf16(jnp.concatenate(columns, axis=1)))
+                for block in range(4):
+                    for k in range(count):
+                        mode_ref[first + k, pl.ds(2 * block + parity, z_devs, stride=8), :] = modes[block * z_devs:(block + 1) * z_devs, k * half:(k + 1) * half]
+                peak = jnp.maximum(peak, jnp.max(jnp.abs(modes), keepdims=True))
         power = jnp.ceil(jnp.log2(peak * (1.0 / CODE_MAX)) + 1e-3)
         gain = jnp.exp2(-power)
         for first in range(0, len(planes), 2):
             count = min(2, len(planes) - first)
-            scaled = [(mode_ref[:, pl.ds((first + k) * half, half)] * gain).reshape(z_devs, 8, half) for k in range(count)]
+            scaled = [(mode_ref[first + k] * gain).reshape(z_devs, 8, half) for k in range(count)]
             codes = jnp.round(jnp.concatenate(scaled, axis=1)).astype(jnp.int32).astype(jnp.int16)
             code_refs[group][:, pl.ds(8 * first, 8 * count), :] = codes
         code_refs[group][:, pl.ds(8 * len(planes), 2), :] = jnp.broadcast_to(power.astype(jnp.int32), (z_devs, 2, half)).astype(jnp.int16)
@@ -227,11 +235,7 @@
     def transform_z(part):
         flat = deq_ref.at[part]
         columns = [flat[pl.ds(ky, grid_n, stride=4), :] for ky in range(4)]
-        zed = dot3((tz_ref[part, 0], tz_ref[part, 1]), split_bf16(jnp.concatenate(columns, axis=1)))
-        if part == 0:
-            zed_ref[...] = zed
-        else:
-            zed_ref[...] += zed
+        return dot3((tz_ref[part, 0], tz_ref[part, 1]), split_bf16(jnp.concatenate(columns, axis=1)))
 
     for acc_ref in acc_refs:
         acc_ref[...] = jnp.zeros_like(acc_ref)
@@ -265,22 +269,24 @@
         deq_ref[part] = decode(0, 2 * part, 2).reshape(rows, half)
     await_codes(1)
     fold(0, decode(1, 0, 2))
-    transform_z(0)
+    zed_ref[...] = transform_z(0)
+    zed_ref[...] += transform_z(1)
     await_codes(2)
-    late = decode(2, 0, 1)
-    fold(1, jnp.concatenate([late, jnp.zeros_like(late)], axis=1))
-    transform_z(1)
-
+    message = recv_refs[2][...].astype(jnp.int32).astype(F32)
+    late_ref[...] = (message[:, :8] * jnp.exp2(message[:, 8:9])).reshape(z_devs * 8, half)
     row = jnp.zeros((8, half), F32)
-    for ky in range(4):
-        cols = pl.ds(ky * half, half)
-        real, imag = zed_ref[pl.ds(0, grid_n), cols], zed_ref[pl.ds(grid_n, grid_n), cols]
-        power = real * real + imag * imag
-        for part in range(2):
-            place = pl.ds(4 * part + ky, half, stride=8)
-            value = bc_ref[place, :] * power[part * half:(part + 1) * half].T
-            ek_ref[place, :] = value
-            row += jnp.sum(value.reshape(half // 8, 8, half), axis=0)
+    for pair in range(2):
+        high, low = split_bf16(jnp.concatenate([late_ref[pl.ds(2 * pair + k, half, stride=4), :] for k in range(2)], axis=1))
+        zed = zed_ref[:, pl.ds(pair * grid_n, grid_n)]
+        zed += jnp.dot(tl_ref[:, pl.ds(0, grid_n)], jnp.concatenate([high, low], axis=0), preferred_element_type=F32)
+        zed += jnp.dot(tl_ref[:, pl.ds(grid_n, half)], high, preferred_element_type=F32)
+        power = zed[:grid_n] * zed[:grid_n] + zed[grid_n:] * zed[grid_n:]
+        for k in range(2):
+            for part in range(2):
+                place = pl.ds(4 * part + 2 * pair + k, half, stride=8)
+                value = bc_ref[place, :] * power[part * half:(part + 1) * half, k * half:(k + 1) * half].T
+                ek_ref[place, :] = value
+                row += jnp.sum(value.reshape(half // 8, 8, half), axis=0)
     row_ref[0] = jnp.broadcast_to(jnp.sum(row, axis=0, keepdims=True), (8, half))
 
     others = rrow_ref.at[pl.ds(0, z_devs - 1), pl.ds(0, 1)]
@@ -312,14 +318,14 @@
         slots = charge.shape[0]
         half = grid_n // 2
         n_groups = len(GROUPS)
-        table_x, table_y, table_z = dft_tables(grid_n, y_devs, z_devs)
+        table_x, table_y, table_z, late_z = dft_tables(grid_n, y_devs, z_devs)
         any_spec = pl.BlockSpec(memory_space=pl.ANY)
         rows = [len(GROUPS[g]) * (grid_n // y_devs) + ghost_rows(g) for g in range(n_groups)]
         codes = [pltpu.VMEM((z_devs, -(-(8 * len(planes) + 2) // 16) * 16, half), jnp.int16) for planes in GROUPS]
         tiles = jnp.swapaxes(influence.reshape(half, 4, 2, half), 1, 2).reshape(8 * half, half)
         mode_energy, energy = pl.pallas_call(
             functools.partial(energy_kernel, y_devs, z_devs),
-            in_specs=[any_spec] * 8,
+            in_specs=[any_spec] * 9,
             out_specs=[pl.BlockSpec(memory_space=pltpu.VMEM), pl.BlockSpec(memory_space=pltpu.SMEM)],
             out_shape=[pltpu.VMEM((8 * half, half), F32), jax.ShapeDtypeStruct((1,), F32)],
             scratch_shapes=[
@@ -327,19 +333,20 @@
                 pltpu.VMEM((2, 2, grid_n, SUB), BF16), pltpu.VMEM((slots, grid_n), BF16), pltpu.VMEM((slots, grid_n), BF16),
                 pltpu.VMEM((2, rows[0], SUB), BF16), pltpu.VMEM((2, rows[0], SUB), BF16),
                 [pltpu.VMEM((r, grid_n), F32) for r in rows], [pltpu.VMEM((r, grid_n), F32) for r in rows],
-                pltpu.VMEM((2 * grid_n, grid_n), F32), pltpu.VMEM((2 * grid_n, grid_n), F32), pltpu.VMEM((2 * grid_n, 4 * half), F32),
+                pltpu.VMEM((2 * grid_n, grid_n), F32), pltpu.VMEM((2 * grid_n, grid_n), F32), pltpu.VMEM((4, 2 * grid_n, half), F32),
                 codes, codes,
                 pltpu.VMEM((2, z_devs * 16, half), F32), pltpu.VMEM((2 * grid_n, 4 * half), F32),
                 pltpu.VMEM((8 * half, half), F32),
-                pltpu.VMEM(table_x.shape[1:], BF16), pltpu.VMEM(table_y.shape, BF16), pltpu.VMEM(table_z.shape, BF16),
+                pltpu.VMEM(table_x.shape[1:], BF16), pltpu.VMEM(table_y.shape, BF16), pltpu.VMEM(table_z.shape, BF16), pltpu.VMEM(late_z.shape, BF16),
+                pltpu.VMEM((z_devs * 8, half), F32),
                 pltpu.VMEM((3, 8, 128), F32), pltpu.VMEM((z_devs, 8, 128), F32),
-                pltpu.SemaphoreType.DMA((2, 4)), pltpu.SemaphoreType.DMA((4,)), pltpu.SemaphoreType.DMA((2, n_groups)),
+                pltpu.SemaphoreType.DMA((2, 4)), pltpu.SemaphoreType.DMA((5,)), pltpu.SemaphoreType.DMA((2, n_groups)),
                 pltpu.SemaphoreType.DMA((n_groups,)), pltpu.SemaphoreType.DMA((n_groups,)),
                 pltpu.SemaphoreType.DMA((4,)),
             ],
             compiler_params=pltpu.CompilerParams(collective_id=0, has_side_effects=True, vmem_limit_bytes=60 * 1024 * 1024),
             name="energy",
-        )(charge.reshape(1, slots), real_mask.reshape(1, slots), grid_idx.T, jnp.transpose(spline_w, (1, 2, 0)), tiles, jnp.asarray(table_x), jnp.asarray(table_y), jnp.asarray(table_z))
+        )(charge.reshape(1, slots), real_mask.reshape(1, slots), grid_idx.T, jnp.transpose(spline_w, (1, 2, 0)), tiles, jnp.asarray(table_x), jnp.asarray(table_y), jnp.asarray(table_z), jnp.asarray(late_z))
         mode_energy = lax.optimization_barrier(0.5 * mode_energy)
         return jnp.swapaxes(mode_energy.reshape(half, 2, 4, half), 1, 2).reshape(influence.shape), energy
 

time: 60.8 us -> 59 us (0.970)
  Pallas kernels: 57.5 us -> 55.7 us
    pallas_call x1, Pallas kernels: 57.5 us -> 55.7 us  [local_energy(): pl.pallas_call(functools.partial(energy_kernel, y_devs, z_devs), in_specs...]
where the time goes in v8:
time: 59 us; the launch traced here: 58.8 us
  Pallas kernels  55.7 us (94%)
  between operations  2.33 us (4%)
  other arithmetic  0.83 us (1%)
    pallas_call x1, Pallas kernels, local_energy(): pl.pallas_call(functools.partial(energy_kernel, y_devs, z_devs), in_specs...  55.7 us

profile of v8, /device:TPU:1, one launch (start us, length us, event | category | flops | bytes accessed | tf_op | source)
XLA Modules:
  0.0 58.8 jit_solution(3248858662624337953)
XLA Ops:
  0.6 55.7 %energy.1 = (f32[1024,128]{1,0:T(8,128)S(1)}, f32[1]{0:T(128)}) custom-call(f32[1,16384]{1,0:T(1,128)} %bitcast.18, s32[1,16384]{1,0:T(1,128)} %bitcast.19, s32[3,16384]{1,0:T(4,128)} %bitcast.17, f32[3,4,16384]{2,1,0:T(4,128)} %bitcast.14, f32[1024,128]{1,0:T(8,128)} %bitcast.16, bf16[2,2,256,256]{3,2,1,0:T(8,128)(2,1)} %constant.10.clone.tx_hbm, ...), custom_call_target="tpu_custom_call" | custom-call | tf_op jit(solution)/shard_map/energy/pallas_call | solution.py:326
  56.3 0.8 %broadcast_multiply_fusion = f32[1024,128]{1,0:T(8,128)} fusion(f32[1024,128]{1,0:T(8,128)S(1)} %get-tuple-element.4), kind=kLoop, calls=%fused_computation | loop fusion | flops 131072 | bytes 1048576 | tf_op jit(solution)/shard_map/mul | solution.py:350

commit v9 on v8

--- a/solution.py
+++ b/solution.py
@@ -13,7 +13,7 @@
 SUB = 512
 CHUNK = 2048
 GROUPS = ((0, 1, 2, 3), (4, 5), (6,))
-STEP_AT = (0, 2, 3)
+STEP_AT = (0, 2, 2)
 EARLY = 2048
 CODE_MAX = 32767.0
 MESH = pl.DeviceIdType.MESH
@@ -76,7 +76,7 @@
 
 
 def energy_kernel(y_devs, z_devs, q_hbm, m_hbm, idx_hbm, w_hbm, bc_hbm, tx_hbm, ty_hbm, tz_hbm, tl_hbm, ek_ref, sum_ref,
-                  q_ref, m_ref, idx_ref, w_ref, near_ref, xh_ref, xl_ref, ph_ref, pl_ref, acc_refs, got_refs, grid_ref, mid_ref, mode_ref,
+                  q_ref, m_ref, idx_ref, w_ref, line_ref, near_ref, xh_ref, xl_ref, ph_ref, pl_ref, acc_refs, got_refs, grid_ref, mid_ref, mode_ref,
                   code_refs, recv_refs,
                   deq_ref, zed_ref, bc_ref, tx_ref, ty_ref, tz_ref, tl_ref, late_ref, row_ref, rrow_ref,
                   early_sem, load_sem, swap_sem, send_sem, recv_sem, row_sem):
@@ -93,9 +93,13 @@
     def chip(step):
         return (my_z + step) & (z_devs - 1)
 
-    def far_first(start):
-        pl.loop(z_devs // 2, z_devs)(start)
-        pl.loop(1, z_devs // 2)(start)
+    def chips_from_far():
+        side = round(z_devs ** (1 / 3))
+        place = [my_z // side ** axis % side for axis in range(3)]
+        there = [[(place[axis] + d) % side * side ** axis for d in range(side)] for axis in range(3)]
+        steps = [(a, b, c) for c in range(side) for b in range(side) for a in range(side)][1:]
+        steps.sort(key=lambda step: -sum(min(d, side - d) for d in step))
+        return [there[0][a] + there[1][b] + there[2][c] for a, b, c in steps]
 
     def slot_loads(piece):
         cols = pl.ds(0, EARLY) if piece == 0 else pl.ds(EARLY, slots - EARLY)
@@ -123,8 +127,7 @@
     def used(group):
         return pl.ds(0, 8 * len(GROUPS[group]) + 2)
 
-    def send(group, step):
-        other = chip(step)
+    def send(group, other):
         return pltpu.make_async_remote_copy(src_ref=code_refs[group].at[other, used(group)], dst_ref=recv_refs[group].at[my_z, used(group)], send_sem=send_sem.at[group], recv_sem=recv_sem.at[group], device_id={'zdom': other}, device_id_type=MESH)
 
     def spread(group, base):
@@ -143,10 +146,12 @@
                 tile_x = (-(ahead >> 4) & 15).astype(F32).astype(BF16)
                 for r in range(grid_n // 16):
                     hit = tile_x == r
-                    near_ref[slot, 0, 16 * r:16 * r + 16, :] = jnp.where(hit, high, zero_16)
-                    near_ref[slot, 1, 16 * r:16 * r + 16, :] = jnp.where(hit, low, zero_16)
-                xh_ref[cols, :] = near_ref[slot, 0].T
-                xl_ref[cols, :] = near_ref[slot, 1].T
+                    line_ref[0, 16 * r:16 * r + 16, :] = jnp.where(hit, high, zero_16)
+                    line_ref[1, 16 * r:16 * r + 16, :] = jnp.where(hit, low, zero_16)
+                for part, far_ref in enumerate((xh_ref, xl_ref)):
+                    turned = line_ref[part].T
+                    near_ref[slot, part] = turned
+                    far_ref[cols, :] = turned
             ahead = row_16 - idx_ref[1:2, cols]
             line_y = pick(ahead, w_ref[1, :, cols])
             tile = -(ahead >> 4)
@@ -169,7 +174,7 @@
             ph_ref[slot, top:top + ghost_rows(group), :] = high
             pl_ref[slot, top:top + ghost_rows(group), :] = low
             if group == 0:
-                part = dot3((ph_ref[slot, rows, :], pl_ref[slot, rows, :]), (near_ref[slot, 0], near_ref[slot, 1]), 1)
+                part = dot3((ph_ref[slot, rows, :], pl_ref[slot, rows, :]), (near_ref[slot, 0], near_ref[slot, 1]))
             else:
                 part = dot3((ph_ref[slot, rows, :], pl_ref[slot, rows, :]), (xh_ref[cols, :], xl_ref[cols, :]))
             total = part if total is None else total + part
@@ -187,14 +192,14 @@
                 block = pl.ds((first + k) * len_y, len_y)
                 ghost = pl.ds(len(planes) * len_y + 8 * (first + k), 8)
                 even, odd = 2 * k * len_y, (2 * k + 1) * len_y
-                grid_ref[pl.ds(even, len_y), :] = acc_ref[block, :] + got_ref[block, :]
-                grid_ref[pl.ds(odd, len_y), :] = sign * (acc_ref[block, :] - got_ref[block, :])
-                grid_ref[pl.ds(even, 8), :] += acc_ref[ghost, :] + got_ref[ghost, :]
-                grid_ref[pl.ds(odd, 8), :] -= sign * (acc_ref[ghost, :] - got_ref[ghost, :])
+                grid_ref[first // 2, pl.ds(even, len_y), :] = acc_ref[block, :] + got_ref[block, :]
+                grid_ref[first // 2, pl.ds(odd, len_y), :] = sign * (acc_ref[block, :] - got_ref[block, :])
+                grid_ref[first // 2, pl.ds(even, 8), :] += acc_ref[ghost, :] + got_ref[ghost, :]
+                grid_ref[first // 2, pl.ds(odd, 8), :] -= sign * (acc_ref[ghost, :] - got_ref[ghost, :])
             size = count * grid_n
-            mid_ref[pl.ds(0, size), :] = dot3(split_bf16(grid_ref[pl.ds(0, size), :]), (tx_ref[0], tx_ref[1]))
+            mid_ref[first // 2, pl.ds(0, size), :] = dot3(split_bf16(grid_ref[first // 2, pl.ds(0, size), :]), (tx_ref[0], tx_ref[1]))
             for parity in range(2):
-                columns = [jnp.concatenate([mid_ref[pl.ds((2 * k + parity) * len_y, len_y), pl.ds(c * half, half)] for c in range(2)], axis=0) for k in range(count)]
+                columns = [jnp.concatenate([mid_ref[first // 2, pl.ds((2 * k + parity) * len_y, len_y), pl.ds(c * half, half)] for c in range(2)], axis=0) for k in range(count)]
                 modes = dot3((ty_ref[parity, 0], ty_ref[parity, 1]), split_bf16(jnp.concatenate(columns, axis=1)))
                 for block in range(4):
                     for k in range(count):
@@ -209,10 +214,13 @@
             code_refs[group][:, pl.ds(8 * first, 8 * count), :] = codes
         code_refs[group][:, pl.ds(8 * len(planes), 2), :] = jnp.broadcast_to(power.astype(jnp.int32), (z_devs, 2, half)).astype(jnp.int16)
 
-        def start(step):
-            send(group, step).start()
-
-        far_first(start)
+        if group < n_groups - 1:
+            @pl.loop(1, z_devs)
+            def _(step):
+                send(group, chip(step)).start()
+        else:
+            for other in chips_from_far():
+                send(group, other).start()
         recv_refs[group][my_z] = code_refs[group][my_z]
 
     def await_all(ref, sem):
@@ -295,10 +303,9 @@
     pair.wait()
     row_ref[2] = row_ref[0] + row_ref[1]
 
-    def start(step):
-        pltpu.make_async_remote_copy(src_ref=row_ref.at[2, pl.ds(0, 1)], dst_ref=rrow_ref.at[my_z, pl.ds(0, 1)], send_sem=row_sem.at[0], recv_sem=row_sem.at[1], device_id={'zdom': chip(step)}, device_id_type=MESH).start()
-
-    far_first(start)
+    for other in chips_from_far():
+        pltpu.make_async_remote_copy(src_ref=row_ref.at[2, pl.ds(0, 1)], dst_ref=rrow_ref.at[my_z, pl.ds(0, 1)], send_sem=row_sem.at[0], recv_sem=row_sem.at[1], device_id={'zdom': other}, device_id_type=MESH).start()
+
     rrow_ref[my_z, pl.ds(0, 1)] = row_ref[2, pl.ds(0, 1)]
     await_all(others, row_sem.at[1])
     sum_ref[0] = jnp.sum(rrow_ref[:, pl.ds(0, 1), :]) * (0.5 / (grid_n * grid_n * grid_n))
@@ -330,10 +337,10 @@
             out_shape=[pltpu.VMEM((8 * half, half), F32), jax.ShapeDtypeStruct((1,), F32)],
             scratch_shapes=[
                 pltpu.VMEM((1, slots), F32), pltpu.VMEM((1, slots), jnp.int32), pltpu.VMEM((3, slots), jnp.int32), pltpu.VMEM((3, 4, slots), F32),
-                pltpu.VMEM((2, 2, grid_n, SUB), BF16), pltpu.VMEM((slots, grid_n), BF16), pltpu.VMEM((slots, grid_n), BF16),
+                pltpu.VMEM((2, grid_n, SUB), BF16), pltpu.VMEM((2, 2, SUB, grid_n), BF16), pltpu.VMEM((slots, grid_n), BF16), pltpu.VMEM((slots, grid_n), BF16),
                 pltpu.VMEM((2, rows[0], SUB), BF16), pltpu.VMEM((2, rows[0], SUB), BF16),
                 [pltpu.VMEM((r, grid_n), F32) for r in rows], [pltpu.VMEM((r, grid_n), F32) for r in rows],
-                pltpu.VMEM((2 * grid_n, grid_n), F32), pltpu.VMEM((2 * grid_n, grid_n), F32), pltpu.VMEM((4, 2 * grid_n, half), F32),
+                pltpu.VMEM((2, 2 * grid_n, grid_n), F32), pltpu.VMEM((2, 2 * grid_n, grid_n), F32), pltpu.VMEM((4, 2 * grid_n, half), F32),
                 codes, codes,
                 pltpu.VMEM((2, z_devs * 16, half), F32), pltpu.VMEM((2 * grid_n, 4 * half), F32),
                 pltpu.VMEM((8 * half, half), F32),

time: 59 us -> 60 us (1.017)
  Pallas kernels: 55.7 us -> 56.7 us
    pallas_call x1, Pallas kernels: 55.7 us -> 56.7 us  [local_energy(): pl.pallas_call(functools.partial(energy_kernel, y_devs, z_devs), in_specs...]
where the time goes in v9:
time: 60 us; the launch traced here: 59.8 us
  Pallas kernels  56.7 us (94%)
  between operations  2.33 us (4%)
  other arithmetic  0.83 us (1%)
    pallas_call x1, Pallas kernels, local_energy(): pl.pallas_call(functools.partial(energy_kernel, y_devs, z_devs), in_specs...  56.7 us

profile of v9, /device:TPU:1, one launch (start us, length us, event | category | flops | bytes accessed | tf_op | source)
XLA Modules:
  0.0 59.8 jit_solution(15381549453431441637)
XLA Ops:
  0.6 56.7 %energy.1 = (f32[1024,128]{1,0:T(8,128)S(1)}, f32[1]{0:T(128)}) custom-call(f32[1,16384]{1,0:T(1,128)} %bitcast.18, s32[1,16384]{1,0:T(1,128)} %bitcast.19, s32[3,16384]{1,0:T(4,128)} %bitcast.17, f32[3,4,16384]{2,1,0:T(4,128)} %bitcast.14, f32[1024,128]{1,0:T(8,128)} %bitcast.16, bf16[2,2,256,256]{3,2,1,0:T(8,128)(2,1)} %constant.10.clone.tx_hbm, ...), custom_call_target="tpu_custom_call" | custom-call | tf_op jit(solution)/shard_map/energy/pallas_call | solution.py:333
  57.3 0.8 %broadcast_multiply_fusion = f32[1024,128]{1,0:T(8,128)} fusion(f32[1024,128]{1,0:T(8,128)S(1)} %get-tuple-element.4), kind=kLoop, calls=%fused_computation | loop fusion | flops 131072 | bytes 1048576 | tf_op jit(solution)/shard_map/mul | solution.py:357

commit v10 on v9

--- a/solution.py
+++ b/solution.py
@@ -13,7 +13,7 @@
 SUB = 512
 CHUNK = 2048
 GROUPS = ((0, 1, 2, 3), (4, 5), (6,))
-STEP_AT = (0, 2, 2)
+STEP_AT = (0, 2, 3)
 EARLY = 2048
 CODE_MAX = 32767.0
 MESH = pl.DeviceIdType.MESH
@@ -93,13 +93,8 @@
     def chip(step):
         return (my_z + step) & (z_devs - 1)
 
-    def chips_from_far():
-        side = round(z_devs ** (1 / 3))
-        place = [my_z // side ** axis % side for axis in range(3)]
-        there = [[(place[axis] + d) % side * side ** axis for d in range(side)] for axis in range(3)]
-        steps = [(a, b, c) for c in range(side) for b in range(side) for a in range(side)][1:]
-        steps.sort(key=lambda step: -sum(min(d, side - d) for d in step))
-        return [there[0][a] + there[1][b] + there[2][c] for a, b, c in steps]
+    def to_chips(start):
+        pl.loop(1, z_devs)(start)
 
     def slot_loads(piece):
         cols = pl.ds(0, EARLY) if piece == 0 else pl.ds(EARLY, slots - EARLY)
@@ -127,7 +122,8 @@
     def used(group):
         return pl.ds(0, 8 * len(GROUPS[group]) + 2)
 
-    def send(group, other):
+    def send(group, step):
+        other = chip(step)
         return pltpu.make_async_remote_copy(src_ref=code_refs[group].at[other, used(group)], dst_ref=recv_refs[group].at[my_z, used(group)], send_sem=send_sem.at[group], recv_sem=recv_sem.at[group], device_id={'zdom': other}, device_id_type=MESH)
 
     def spread(group, base):
@@ -214,13 +210,10 @@
             code_refs[group][:, pl.ds(8 * first, 8 * count), :] = codes
         code_refs[group][:, pl.ds(8 * len(planes), 2), :] = jnp.broadcast_to(power.astype(jnp.int32), (z_devs, 2, half)).astype(jnp.int16)
 
-        if group < n_groups - 1:
-            @pl.loop(1, z_devs)
-            def _(step):
-                send(group, chip(step)).start()
-        else:
-            for other in chips_from_far():
-                send(group, other).start()
+        def start(step):
+            send(group, step).start()
+
+        to_chips(start)
         recv_refs[group][my_z] = code_refs[group][my_z]
 
     def await_all(ref, sem):
@@ -303,9 +296,10 @@
     pair.wait()
     row_ref[2] = row_ref[0] + row_ref[1]
 
-    for other in chips_from_far():
-        pltpu.make_async_remote_copy(src_ref=row_ref.at[2, pl.ds(0, 1)], dst_ref=rrow_ref.at[my_z, pl.ds(0, 1)], send_sem=row_sem.at[0], recv_sem=row_sem.at[1], device_id={'zdom': other}, device_id_type=MESH).start()
-
+    def start(step):
+        pltpu.make_async_remote_copy(src_ref=row_ref.at[2, pl.ds(0, 1)], dst_ref=rrow_ref.at[my_z, pl.ds(0, 1)], send_sem=row_sem.at[0], recv_sem=row_sem.at[1], device_id={'zdom': chip(step)}, device_id_type=MESH).start()
+
+    to_chips(start)
     rrow_ref[my_z, pl.ds(0, 1)] = row_ref[2, pl.ds(0, 1)]
     await_all(others, row_sem.at[1])
     sum_ref[0] = jnp.sum(rrow_ref[:, pl.ds(0, 1), :]) * (0.5 / (grid_n * grid_n * grid_n))

time: 60 us -> 60 us (level)
  no operation moved by 1% of the time
where the time goes in v10:
time: 60 us; the launch traced here: 59.9 us
  Pallas kernels  56.7 us (94%)
  between operations  2.33 us (4%)
  other arithmetic  0.83 us (1%)
    pallas_call x1, Pallas kernels, local_energy(): pl.pallas_call(functools.partial(energy_kernel, y_devs, z_devs), in_specs...  56.7 us

profile of v10, /device:TPU:1, one launch (start us, length us, event | category | flops | bytes accessed | tf_op | source)
XLA Modules:
  0.0 59.9 jit_solution(12693965590604668978)
XLA Ops:
  0.6 56.7 %energy.1 = (f32[1024,128]{1,0:T(8,128)S(1)}, f32[1]{0:T(128)}) custom-call(f32[1,16384]{1,0:T(1,128)} %bitcast.18, s32[1,16384]{1,0:T(1,128)} %bitcast.19, s32[3,16384]{1,0:T(4,128)} %bitcast.17, f32[3,4,16384]{2,1,0:T(4,128)} %bitcast.14, f32[1024,128]{1,0:T(8,128)} %bitcast.16, bf16[2,2,256,256]{3,2,1,0:T(8,128)(2,1)} %constant.10.clone.tx_hbm, ...), custom_call_target="tpu_custom_call" | custom-call | tf_op jit(solution)/shard_map/energy/pallas_call | solution.py:327
  57.4 0.8 %broadcast_multiply_fusion = f32[1024,128]{1,0:T(8,128)} fusion(f32[1024,128]{1,0:T(8,128)S(1)} %get-tuple-element.4), kind=kLoop, calls=%fused_computation | loop fusion | flops 131072 | bytes 1048576 | tf_op jit(solution)/shard_map/mul | solution.py:351

commit v11 on v10

--- a/solution.py
+++ b/solution.py
@@ -93,8 +93,9 @@
     def chip(step):
         return (my_z + step) & (z_devs - 1)
 
-    def to_chips(start):
-        pl.loop(1, z_devs)(start)
+    def far_first(start):
+        pl.loop(z_devs // 2, z_devs)(start)
+        pl.loop(1, z_devs // 2)(start)
 
     def slot_loads(piece):
         cols = pl.ds(0, EARLY) if piece == 0 else pl.ds(EARLY, slots - EARLY)
@@ -213,7 +214,7 @@
         def start(step):
             send(group, step).start()
 
-        to_chips(start)
+        far_first(start)
         recv_refs[group][my_z] = code_refs[group][my_z]
 
     def await_all(ref, sem):
@@ -299,7 +300,7 @@
     def start(step):
         pltpu.make_async_remote_copy(src_ref=row_ref.at[2, pl.ds(0, 1)], dst_ref=rrow_ref.at[my_z, pl.ds(0, 1)], send_sem=row_sem.at[0], recv_sem=row_sem.at[1], device_id={'zdom': chip(step)}, device_id_type=MESH).start()
 
-    to_chips(start)
+    far_first(start)
     rrow_ref[my_z, pl.ds(0, 1)] = row_ref[2, pl.ds(0, 1)]
     await_all(others, row_sem.at[1])
     sum_ref[0] = jnp.sum(rrow_ref[:, pl.ds(0, 1), :]) * (0.5 / (grid_n * grid_n * grid_n))

time: 60 us -> 59.6 us (level)
  no operation moved by 1% of the time
where the time goes in v11:
time: 59.6 us; the launch traced here: 59.4 us
  Pallas kernels  56.3 us (94%)
  between operations  2.33 us (4%)
  other arithmetic  0.83 us (1%)
    pallas_call x1, Pallas kernels, local_energy(): pl.pallas_call(functools.partial(energy_kernel, y_devs, z_devs), in_specs...  56.3 us

profile of v11, /device:TPU:1, one launch (start us, length us, event | category | flops | bytes accessed | tf_op | source)
XLA Modules:
  0.0 59.4 jit_solution(16754769760530293721)
XLA Ops:
  0.6 56.3 %energy.1 = (f32[1024,128]{1,0:T(8,128)S(1)}, f32[1]{0:T(128)}) custom-call(f32[1,16384]{1,0:T(1,128)} %bitcast.18, s32[1,16384]{1,0:T(1,128)} %bitcast.19, s32[3,16384]{1,0:T(4,128)} %bitcast.17, f32[3,4,16384]{2,1,0:T(4,128)} %bitcast.14, f32[1024,128]{1,0:T(8,128)} %bitcast.16, bf16[2,2,256,256]{3,2,1,0:T(8,128)(2,1)} %constant.10.clone.tx_hbm, ...), custom_call_target="tpu_custom_call" | custom-call | tf_op jit(solution)/shard_map/energy/pallas_call | solution.py:328
  56.9 0.8 %broadcast_multiply_fusion = f32[1024,128]{1,0:T(8,128)} fusion(f32[1024,128]{1,0:T(8,128)S(1)} %get-tuple-element.4), kind=kLoop, calls=%fused_computation | loop fusion | flops 131072 | bytes 1048576 | tf_op jit(solution)/shard_map/mul | solution.py:352

commit v12 on v8

--- a/solution.py
+++ b/solution.py
@@ -13,7 +13,7 @@
 SUB = 512
 CHUNK = 2048
 GROUPS = ((0, 1, 2, 3), (4, 5), (6,))
-STEP_AT = (0, 2, 3)
+STEP_AT = (0, 1, 2)
 EARLY = 2048
 CODE_MAX = 32767.0
 MESH = pl.DeviceIdType.MESH

time: 59 us -> 59 us (level)
  no operation moved by 1% of the time
where the time goes in v12:
time: 59 us; the launch traced here: 58.8 us
  Pallas kernels  55.7 us (94%)
  between operations  2.33 us (4%)
  other arithmetic  0.83 us (1%)
    pallas_call x1, Pallas kernels, local_energy(): pl.pallas_call(functools.partial(energy_kernel, y_devs, z_devs), in_specs...  55.7 us

profile of v12, /device:TPU:1, one launch (start us, length us, event | category | flops | bytes accessed | tf_op | source)
XLA Modules:
  0.0 58.8 jit_solution(10134467255101963466)
XLA Ops:
  0.6 55.7 %energy.1 = (f32[1024,128]{1,0:T(8,128)S(1)}, f32[1]{0:T(128)}) custom-call(f32[1,16384]{1,0:T(1,128)} %bitcast.18, s32[1,16384]{1,0:T(1,128)} %bitcast.19, s32[3,16384]{1,0:T(4,128)} %bitcast.17, f32[3,4,16384]{2,1,0:T(4,128)} %bitcast.14, f32[1024,128]{1,0:T(8,128)} %bitcast.16, bf16[2,2,256,256]{3,2,1,0:T(8,128)(2,1)} %constant.10.clone.tx_hbm, ...), custom_call_target="tpu_custom_call" | custom-call | tf_op jit(solution)/shard_map/energy/pallas_call | solution.py:326
  56.3 0.8 %broadcast_multiply_fusion = f32[1024,128]{1,0:T(8,128)} fusion(f32[1024,128]{1,0:T(8,128)S(1)} %get-tuple-element.4), kind=kLoop, calls=%fused_computation | loop fusion | flops 131072 | bytes 1048576 | tf_op jit(solution)/shard_map/mul | solution.py:350

commit v13 on v8

--- a/solution.py
+++ b/solution.py
@@ -94,8 +94,8 @@
         return (my_z + step) & (z_devs - 1)
 
     def far_first(start):
-        pl.loop(z_devs // 2, z_devs)(start)
-        pl.loop(1, z_devs // 2)(start)
+        for first in (2, 1, 3, 0):
+            pl.loop(max(1, first * z_devs // 4), (first + 1) * z_devs // 4)(start)
 
     def slot_loads(piece):
         cols = pl.ds(0, EARLY) if piece == 0 else pl.ds(EARLY, slots - EARLY)

time: 59 us -> 59 us (level)
  no operation moved by 1% of the time
where the time goes in v13:
time: 59 us; the launch traced here: 58.9 us
  Pallas kernels  55.7 us (94%)
  between operations  2.33 us (4%)
  other arithmetic  0.83 us (1%)
    pallas_call x1, Pallas kernels, local_energy(): pl.pallas_call(functools.partial(energy_kernel, y_devs, z_devs), in_specs...  55.7 us

profile of v13, /device:TPU:1, one launch (start us, length us, event | category | flops | bytes accessed | tf_op | source)
XLA Modules:
  0.0 58.9 jit_solution(18045070779372675095)
XLA Ops:
  0.6 55.7 %energy.1 = (f32[1024,128]{1,0:T(8,128)S(1)}, f32[1]{0:T(128)}) custom-call(f32[1,16384]{1,0:T(1,128)} %bitcast.18, s32[1,16384]{1,0:T(1,128)} %bitcast.19, s32[3,16384]{1,0:T(4,128)} %bitcast.17, f32[3,4,16384]{2,1,0:T(4,128)} %bitcast.14, f32[1024,128]{1,0:T(8,128)} %bitcast.16, bf16[2,2,256,256]{3,2,1,0:T(8,128)(2,1)} %constant.10.clone.tx_hbm, ...), custom_call_target="tpu_custom_call" | custom-call | tf_op jit(solution)/shard_map/energy/pallas_call | solution.py:326
  56.4 0.8 %broadcast_multiply_fusion = f32[1024,128]{1,0:T(8,128)} fusion(f32[1024,128]{1,0:T(8,128)S(1)} %get-tuple-element.4), kind=kLoop, calls=%fused_computation | loop fusion | flops 131072 | bytes 1048576 | tf_op jit(solution)/shard_map/mul | solution.py:350

commit v14 on v8

--- a/solution.py
+++ b/solution.py
@@ -108,7 +108,8 @@
 
     @pl.loop(1, z_devs)
     def _(step):
-        pl.semaphore_signal(barrier, inc=1, device_id={'zdom': chip(step)}, device_id_type=MESH)
+        for core in range(y_devs):
+            pl.semaphore_signal(barrier, inc=1, device_id={'zdom': chip(step), 'ydom': core}, device_id_type=MESH)
 
     pl.semaphore_signal(barrier, inc=1, device_id=partner, device_id_type=MESH)
 
@@ -257,7 +258,7 @@
                     transform_send(group - 1)
 
         if group == 0:
-            pl.semaphore_wait(barrier, z_devs)
+            pl.semaphore_wait(barrier, y_devs * z_devs - 1)
             for load in loads:
                 load.wait()
         swap(group).start()
@@ -289,17 +290,19 @@
                 row += jnp.sum(value.reshape(half // 8, 8, half), axis=0)
     row_ref[0] = jnp.broadcast_to(jnp.sum(row, axis=0, keepdims=True), (8, half))
 
-    others = rrow_ref.at[pl.ds(0, z_devs - 1), pl.ds(0, 1)]
-    pair = pltpu.make_async_remote_copy(src_ref=row_ref.at[0, pl.ds(0, 1)], dst_ref=row_ref.at[1, pl.ds(0, 1)], send_sem=row_sem.at[2], recv_sem=row_sem.at[3], device_id=partner, device_id_type=MESH)
-    pair.start()
-    pair.wait()
-    row_ref[2] = row_ref[0] + row_ref[1]
+    me = my_z * y_devs + my_y
+    others = rrow_ref.at[pl.ds(0, y_devs * z_devs - 1), pl.ds(0, 1)]
+
+    def row_copy(device):
+        return pltpu.make_async_remote_copy(src_ref=row_ref.at[0, pl.ds(0, 1)], dst_ref=rrow_ref.at[me, pl.ds(0, 1)], send_sem=row_sem.at[0], recv_sem=row_sem.at[1], device_id=device, device_id_type=MESH)
 
     def start(step):
-        pltpu.make_async_remote_copy(src_ref=row_ref.at[2, pl.ds(0, 1)], dst_ref=rrow_ref.at[my_z, pl.ds(0, 1)], send_sem=row_sem.at[0], recv_sem=row_sem.at[1], device_id={'zdom': chip(step)}, device_id_type=MESH).start()
+        for core in range(y_devs):
+            row_copy({'zdom': chip(step), 'ydom': core}).start()
 
     far_first(start)
-    rrow_ref[my_z, pl.ds(0, 1)] = row_ref[2, pl.ds(0, 1)]
+    row_copy(partner).start()
+    rrow_ref[me, pl.ds(0, 1)] = row_ref[0, pl.ds(0, 1)]
     await_all(others, row_sem.at[1])
     sum_ref[0] = jnp.sum(rrow_ref[:, pl.ds(0, 1), :]) * (0.5 / (grid_n * grid_n * grid_n))
     await_all(others, row_sem.at[0])
@@ -339,7 +342,7 @@
                 pltpu.VMEM((8 * half, half), F32),
                 pltpu.VMEM(table_x.shape[1:], BF16), pltpu.VMEM(table_y.shape, BF16), pltpu.VMEM(table_z.shape, BF16), pltpu.VMEM(late_z.shape, BF16),
                 pltpu.VMEM((z_devs * 8, half), F32),
-                pltpu.VMEM((3, 8, 128), F32), pltpu.VMEM((z_devs, 8, 128), F32),
+                pltpu.VMEM((3, 8, 128), F32), pltpu.VMEM((y_devs * z_devs, 8, 128), F32),
                 pltpu.SemaphoreType.DMA((2, 4)), pltpu.SemaphoreType.DMA((5,)), pltpu.SemaphoreType.DMA((2, n_groups)),
                 pltpu.SemaphoreType.DMA((n_groups,)), pltpu.SemaphoreType.DMA((n_groups,)),
                 pltpu.SemaphoreType.DMA((4,)),

time: 59 us -> 58.9 us (level)
  no operation moved by 1% of the time
where the time goes in v14:
time: 58.9 us; the launch traced here: 58.8 us
  Pallas kernels  55.6 us (94%)
  between operations  2.33 us (4%)
  other arithmetic  0.83 us (1%)
    pallas_call x1, Pallas kernels, local_energy(): pl.pallas_call(functools.partial(energy_kernel, y_devs, z_devs), in_specs...  55.6 us

profile of v14, /device:TPU:1, one launch (start us, length us, event | category | flops | bytes accessed | tf_op | source)
XLA Modules:
  0.0 58.8 jit_solution(3353449647324888452)
XLA Ops:
  0.6 55.6 %energy.1 = (f32[1024,128]{1,0:T(8,128)S(1)}, f32[1]{0:T(128)}) custom-call(f32[1,16384]{1,0:T(1,128)} %bitcast.18, s32[1,16384]{1,0:T(1,128)} %bitcast.19, s32[3,16384]{1,0:T(4,128)} %bitcast.17, f32[3,4,16384]{2,1,0:T(4,128)} %bitcast.14, f32[1024,128]{1,0:T(8,128)} %bitcast.16, bf16[2,2,256,256]{3,2,1,0:T(8,128)(2,1)} %constant.10.clone.tx_hbm, ...), custom_call_target="tpu_custom_call" | custom-call | tf_op jit(solution)/shard_map/energy/pallas_call | solution.py:329
  56.3 0.8 %broadcast_multiply_fusion = f32[1024,128]{1,0:T(8,128)} fusion(f32[1024,128]{1,0:T(8,128)S(1)} %get-tuple-element.4), kind=kLoop, calls=%fused_computation | loop fusion | flops 131072 | bytes 1048576 | tf_op jit(solution)/shard_map/mul | solution.py:353

commit v15 on v14

--- a/solution.py
+++ b/solution.py
@@ -102,9 +102,8 @@
         return [pltpu.make_async_copy(hbm.at[lead + (cols,)], ref.at[lead + (cols,)], early_sem.at[piece, k])
                 for k, (hbm, ref, lead) in enumerate(((q_hbm, q_ref, (slice(None),)), (m_hbm, m_ref, (slice(None),)), (idx_hbm, idx_ref, (slice(None),)), (w_hbm, w_ref, (slice(None), slice(None)))))]
 
-    for piece in range(2):
-        for load in slot_loads(piece):
-            load.start()
+    for load in slot_loads(0):
+        load.start()
 
     @pl.loop(1, z_devs)
     def _(step):
@@ -115,7 +114,7 @@
 
     loads = [pltpu.make_async_copy(tx_hbm.at[my_y], tx_ref, load_sem.at[0]), pltpu.make_async_copy(ty_hbm, ty_ref, load_sem.at[1]),
              pltpu.make_async_copy(tz_hbm, tz_ref, load_sem.at[2]), pltpu.make_async_copy(bc_hbm, bc_ref, load_sem.at[3]), pltpu.make_async_copy(tl_hbm, tl_ref, load_sem.at[4])]
-    for load in loads:
+    for load in slot_loads(1) + loads:
         load.start()
 
     def swap(group):
@@ -188,14 +187,14 @@
                 block = pl.ds((first + k) * len_y, len_y)
                 ghost = pl.ds(len(planes) * len_y + 8 * (first + k), 8)
                 even, odd = 2 * k * len_y, (2 * k + 1) * len_y
-                grid_ref[pl.ds(even, len_y), :] = acc_ref[block, :] + got_ref[block, :]
-                grid_ref[pl.ds(odd, len_y), :] = sign * (acc_ref[block, :] - got_ref[block, :])
-                grid_ref[pl.ds(even, 8), :] += acc_ref[ghost, :] + got_ref[ghost, :]
-                grid_ref[pl.ds(odd, 8), :] -= sign * (acc_ref[ghost, :] - got_ref[ghost, :])
+                grid_ref[first // 2, pl.ds(even, len_y), :] = acc_ref[block, :] + got_ref[block, :]
+                grid_ref[first // 2, pl.ds(odd, len_y), :] = sign * (acc_ref[block, :] - got_ref[block, :])
+                grid_ref[first // 2, pl.ds(even, 8), :] += acc_ref[ghost, :] + got_ref[ghost, :]
+                grid_ref[first // 2, pl.ds(odd, 8), :] -= sign * (acc_ref[ghost, :] - got_ref[ghost, :])
             size = count * grid_n
-            mid_ref[pl.ds(0, size), :] = dot3(split_bf16(grid_ref[pl.ds(0, size), :]), (tx_ref[0], tx_ref[1]))
+            mid_ref[first // 2, pl.ds(0, size), :] = dot3(split_bf16(grid_ref[first // 2, pl.ds(0, size), :]), (tx_ref[0], tx_ref[1]))
             for parity in range(2):
-                columns = [jnp.concatenate([mid_ref[pl.ds((2 * k + parity) * len_y, len_y), pl.ds(c * half, half)] for c in range(2)], axis=0) for k in range(count)]
+                columns = [jnp.concatenate([mid_ref[first // 2, pl.ds((2 * k + parity) * len_y, len_y), pl.ds(c * half, half)] for c in range(2)], axis=0) for k in range(count)]
                 modes = dot3((ty_ref[parity, 0], ty_ref[parity, 1]), split_bf16(jnp.concatenate(columns, axis=1)))
                 for block in range(4):
                     for k in range(count):
@@ -336,7 +335,7 @@
                 pltpu.VMEM((2, 2, grid_n, SUB), BF16), pltpu.VMEM((slots, grid_n), BF16), pltpu.VMEM((slots, grid_n), BF16),
                 pltpu.VMEM((2, rows[0], SUB), BF16), pltpu.VMEM((2, rows[0], SUB), BF16),
                 [pltpu.VMEM((r, grid_n), F32) for r in rows], [pltpu.VMEM((r, grid_n), F32) for r in rows],
-                pltpu.VMEM((2 * grid_n, grid_n), F32), pltpu.VMEM((2 * grid_n, grid_n), F32), pltpu.VMEM((4, 2 * grid_n, half), F32),
+                pltpu.VMEM((2, 2 * grid_n, grid_n), F32), pltpu.VMEM((2, 2 * grid_n, grid_n), F32), pltpu.VMEM((4, 2 * grid_n, half), F32),
                 codes, codes,
                 pltpu.VMEM((2, z_devs * 16, half), F32), pltpu.VMEM((2 * grid_n, 4 * half), F32),
                 pltpu.VMEM((8 * half, half), F32),

time: 58.9 us -> 59 us (level)
  no operation moved by 1% of the time
where the time goes in v15:
time: 59 us; the launch traced here: 58.8 us
  Pallas kernels  55.7 us (94%)
  between operations  2.33 us (4%)
  other arithmetic  0.83 us (1%)
    pallas_call x1, Pallas kernels, local_energy(): pl.pallas_call(functools.partial(energy_kernel, y_devs, z_devs), in_specs...  55.7 us

profile of v15, /device:TPU:1, one launch (start us, length us, event | category | flops | bytes accessed | tf_op | source)
XLA Modules:
  0.0 58.8 jit_solution(4740906695719849272)
XLA Ops:
  0.6 55.7 %energy.1 = (f32[1024,128]{1,0:T(8,128)S(1)}, f32[1]{0:T(128)}) custom-call(f32[1,16384]{1,0:T(1,128)} %bitcast.18, s32[1,16384]{1,0:T(1,128)} %bitcast.19, s32[3,16384]{1,0:T(4,128)} %bitcast.17, f32[3,4,16384]{2,1,0:T(4,128)} %bitcast.14, f32[1024,128]{1,0:T(8,128)} %bitcast.16, bf16[2,2,256,256]{3,2,1,0:T(8,128)(2,1)} %constant.10.clone.tx_hbm, ...), custom_call_target="tpu_custom_call" | custom-call | tf_op jit(solution)/shard_map/energy/pallas_call | solution.py:328
  56.3 0.8 %broadcast_multiply_fusion = f32[1024,128]{1,0:T(8,128)} fusion(f32[1024,128]{1,0:T(8,128)S(1)} %get-tuple-element.4), kind=kLoop, calls=%fused_computation | loop fusion | flops 131072 | bytes 1048576 | tf_op jit(solution)/shard_map/mul | solution.py:352
